TPU v7x, 16 devices: a whole 2x2x2 slice. The times are simulated.
16 devices in a mesh: rep: 1, dp: 16 (over x, y, z, core).
Axes of the slice: x: 2, y: 2, z: 2, core: 2. Of those that a mesh axis runs over, the one named last changes fastest.
Arguments:
- x: bfloat16 [16, 2048, 1280], P(('rep', 'dp'))
- dy: bfloat16 [16, 2048, 1280], P(('rep', 'dp'))
- w_gate: bfloat16 [2, 1280, 3072], P(None, 'dp')
- w_up: bfloat16 [2, 1280, 3072], P(None, 'dp')
- w_down: bfloat16 [2, 3072, 1280], P(None, 'dp')
- m_w_gate: float32 [2, 1280, 3072], P(None, 'dp')
- m_w_up: float32 [2, 1280, 3072], P(None, 'dp')
- m_w_down: float32 [2, 3072, 1280], P(None, 'dp')
- v_w_gate: float32 [2, 1280, 3072], P(None, 'dp')
- v_w_up: float32 [2, 1280, 3072], P(None, 'dp')
- v_w_down: float32 [2, 3072, 1280], P(None, 'dp')
Outputs:
- output 1: bfloat16 [2, 1280, 3072], P('rep', 'dp')
- output 2: bfloat16 [2, 1280, 3072], P('rep', 'dp')
- output 3: bfloat16 [2, 3072, 1280], P('rep', 'dp')
- output 4: float32 [2, 1280, 3072], P('rep', 'dp')
- output 5: float32 [2, 1280, 3072], P('rep', 'dp')
- output 6: float32 [2, 3072, 1280], P('rep', 'dp')
- output 7: float32 [2, 1280, 3072], P('rep', 'dp')
- output 8: float32 [2, 1280, 3072], P('rep', 'dp')
- output 9: float32 [2, 3072, 1280], P('rep', 'dp')
All inputs are finite; a program needn't handle non-finite values.
Results may differ from a plain program's by a relative error of at most 0.022.
Values are sent between devices in bfloat16 or wider.
A program may use at most 2 GiB of HBM per device.

v0:
```python
import jax
import jax.numpy as jnp
from jax import lax
from jax.sharding import PartitionSpec as P

NAMES = ("w_gate", "w_up", "w_down")


def matmul(a, w):
    return jnp.dot(a, w, preferred_element_type=jnp.float32).astype(jnp.bfloat16)


def normed(h):
    wide = h.astype(jnp.float32)
    scale = lax.rsqrt(jnp.mean(wide**2, -1, keepdims=True) + 1e-6)
    return (wide * scale).astype(jnp.bfloat16)


def layer(h, w):
    a = normed(h)
    gate = jnp.dot(a, w["w_gate"], preferred_element_type=jnp.float32)
    up = jnp.dot(a, w["w_up"], preferred_element_type=jnp.float32)
    return h + matmul((jax.nn.silu(gate) * up).astype(jnp.bfloat16), w["w_down"])


def adamw(w, m, v, g):
    m = 0.9 * m + 0.1 * g
    v = 0.95 * v + 0.05 * g * g
    step = m * lax.rsqrt(v + 1e-8) + 0.1 * w
    return (w - 0.02 * step).astype(jnp.bfloat16), m, v


def clipped(gradients, sum_of_squares, count):
    factor = jnp.minimum(1.0, 0.5 * lax.rsqrt(sum_of_squares / count + 1e-30))
    return [g * factor for g in gradients]


def solution(mesh):
    def fetched(weights, number):
        return {name: lax.all_gather(w[number], "dp", axis=0, tiled=True) for name, w in zip(NAMES, weights, strict=True)}

    def step(x, dy, *arrays):
        weights, m, v = (arrays[i : i + 3] for i in (0, 3, 6))
        layers = weights[0].shape[0]
        h, kept = x[0], []
        for number in range(layers):
            kept.append(h)
            h = layer(h, fetched(weights, number))
        by_h, mine = dy[0], [None] * layers
        for number in reversed(range(layers)):
            _, back = jax.vjp(lambda w, h: layer(h, w), fetched(weights, number), kept[number])
            by_w, by_h = back(by_h)
            mine[number] = [lax.psum_scatter(by_w[name], "dp", scatter_dimension=0, tiled=True) for name in NAMES]
        gradients = [jnp.stack([mine[number][i] for number in range(layers)]).astype(jnp.float32) for i in range(3)]
        squares = lax.psum(sum(jnp.sum(g * g) for g in gradients), "dp")
        gradients = clipped(gradients, squares, lax.psum(1, "dp") * sum(g.size for g in gradients))
        new = [adamw(w.astype(jnp.float32), m, v, g) for w, m, v, g in zip(weights, m, v, gradients, strict=True)]
        return tuple(one[which] for which in range(3) for one in new)

    states, cut = P(("rep", "dp"), None, None), P(None, "dp", None)
    return jax.shard_map(
        step,
        mesh=mesh,
        in_specs=(states, states) + (cut,) * 9,
        out_specs=(P("rep", "dp", None),) * 9,
        check_vma=False,
    )
```

profile of v0, /device:TPU:0, one launch (start us, length us, event | category | flops | bytes accessed | tf_op | source)
XLA Modules:
  0.0 949.5 jit_solution(8598383954629235639)
XLA Ops:
  7.2 0.0 all-gather.13.cloned.1.call-start
  7.2 2.2 fusion.105
  9.4 0.0 all-gather.13.cloned.1.call-update
  9.4 0.0 all-gather.15.cloned.1.call-start
  9.5 2.2 fusion.104
  11.7 0.0 all-gather.15.cloned.1.call-update
  11.7 0.0 all-gather.17.cloned.1.call-start
  11.7 2.2 fusion.103
  13.9 0.0 all-gather.17.cloned.1.call-update
  13.9 0.0 all-gather.21.cloned.1.call-start
  14.0 0.5 all-gather.21.cloned.1.call-update
  14.5 0.0 all-gather.23.cloned.1.call-start
  14.6 0.5 all-gather.23.cloned.1.call-update
  15.1 0.0 all-gather.19.cloned.1.call-start
  15.2 0.5 all-gather.19.cloned.1.call-update
  15.7 0.0 reduce-scatter.15.cloned.1.call-start
  15.7 7.9 copy.20
  23.7 3.6 fusion.21
  27.3 7.9 copy.21
  35.2 25.3 %all-gather.13.cloned.1.call-done = bf16[1,1280,3072]{2,1,0:T(8,128)(2,1)} async-done(((bf16[1,80,3072]{2,1,0:T(8,128)(2,1)}), bf16[1,1280,3072]{2,1,0:T(8,128)(2,1)}) %all-gather.13.cloned.1.call-update) | async-done | bytes 7864336 | tf_op jit(solution)/shard_map/all_gather | solution.py:40
  60.6 23.4 %fusion.41 = f32[2048,3072]{1,0:T(8,128)} fusion(bf16[1,1280,3072]{2,1,0:T(8,128)(2,1)} %all-gather.13.cloned.1.call-done, bf16[1,2048,1280]{1,2,0:T(8,128)(2,1)} %copy.20, f32[2048]{0:T(1024)S(1)} %add_rsqrt_fusion), kind=kOutput, calls=%fused_computation.59 | convolution fusion | flops 16113991680 | bytes 38281216 | tf_op jit(solution)/shard_map/dot_general | solution.py:21
  84.0 26.3 %all-gather.15.cloned.1.call-done = bf16[1,1280,3072]{2,1,0:T(8,128)(2,1)} async-done(((bf16[1,80,3072]{2,1,0:T(8,128)(2,1)}), bf16[1,1280,3072]{2,1,0:T(8,128)(2,1)}) %all-gather.15.cloned.1.call-update) | async-done | bytes 7864336 | tf_op jit(solution)/shard_map/all_gather | solution.py:40
  110.3 34.5 %multiply_convert_fusion.1 = (bf16[2048,3072]{1,0:T(8,128)(2,1)}, f32[2048,3072]{1,0:T(8,128)}) fusion(f32[2048,3072]{1,0:T(8,128)} %fusion.41, bf16[1,1280,3072]{2,1,0:T(8,128)(2,1)} %all-gather.15.cloned.1.call-done, bf16[1,2048,1280]{1,2,0:T(8,128)(2,1)} %copy.20, f32[2048]{0:T(1024)S(1)} %add_rsqrt_fusion), kind=kOutput, calls=%fused_computation.17 | convolution fusion | flops 16151740416 | bytes 76029952 | tf_op jit(solution)/shard_map/dot_general | solution.py:22
  144.8 15.2 %all-gather.17.cloned.1.call-done = bf16[1,3072,1280]{2,1,0:T(8,128)(2,1)} async-done(((bf16[1,192,1280]{2,1,0:T(8,128)(2,1)}), bf16[1,3072,1280]{2,1,0:T(8,128)(2,1)}) %all-gather.17.cloned.1.call-update) | async-done | bytes 7864336 | tf_op jit(solution)/shard_map/all_gather | solution.py:40
  160.1 23.7 %fusion.25 = (f32[2048]{0:T(1024)S(1)}, bf16[2048,1280]{0,1:T(8,128)(2,1)}) fusion(bf16[2048,3072]{1,0:T(8,128)(2,1)} %get-tuple-element.24, bf16[1,3072,1280]{2,1,0:T(8,128)(2,1)} %all-gather.17.cloned.1.call-done, bf16[1,2048,1280]{1,2,0:T(8,128)(2,1)} %copy.20), kind=kOutput, calls=%fused_computation.43 | convolution fusion | flops 16119232512 | bytes 30941184 | tf_op jit(solution)/shard_map/dot_general | solution.py:10
  183.7 0.6 copy-done.14
  184.3 25.3 %all-gather.21.cloned.1.call-done = bf16[1,3072,1280]{2,1,0:T(8,128)(2,1)} async-done(((bf16[1,192,1280]{2,1,0:T(8,128)(2,1)}), bf16[1,3072,1280]{2,1,0:T(8,128)(2,1)}) %all-gather.21.cloned.1.call-update) | async-done | bytes 7864336 | tf_op jit(solution)/shard_map/all_gather | solution.py:40
  209.7 22.8 %convolution_convert_fusion.2 = bf16[2048,3072]{1,0:T(8,128)(2,1)} fusion(bf16[1,3072,1280]{2,1,0:T(8,128)(2,1)} %all-gather.21.cloned.1.call-done, bf16[1,2048,1280]{2,1,0:T(8,128)(2,1)} %param.12), kind=kOutput, calls=%fused_computation.36 | convolution fusion | flops 16112418816 | bytes 25690112 | tf_op jit(solution)/shard_map/transpose(jvp())/dot_general | solution.py:10
  232.5 26.8 %all-gather.23.cloned.1.call-done = bf16[1,1280,3072]{2,1,0:T(8,128)(2,1)} async-done(((bf16[1,80,3072]{2,1,0:T(8,128)(2,1)}), bf16[1,1280,3072]{2,1,0:T(8,128)(2,1)}) %all-gather.23.cloned.1.call-update) | async-done | bytes 7864336 | tf_op jit(solution)/shard_map/all_gather | solution.py:40
  259.2 23.5 %fusion.28 = f32[2048,3072]{1,0:T(8,128)} fusion(bf16[1,1280,3072]{2,1,0:T(8,128)(2,1)} %all-gather.23.cloned.1.call-done, bf16[2048,1280]{0,1:T(8,128)(2,1)} %get-tuple-element.27, f32[2048]{0:T(1024)S(1)} %fusion.91), kind=kOutput, calls=%fused_computation.46 | convolution fusion | flops 16113991680 | bytes 38281216 | tf_op jit(solution)/shard_map/jvp()/dot_general | solution.py:22
  282.7 26.1 %all-gather.19.cloned.1.call-done = bf16[1,1280,3072]{2,1,0:T(8,128)(2,1)} async-done(((bf16[1,80,3072]{2,1,0:T(8,128)(2,1)}), bf16[1,1280,3072]{2,1,0:T(8,128)(2,1)}) %all-gather.19.cloned.1.call-update) | async-done | bytes 7864336 | tf_op jit(solution)/shard_map/all_gather | solution.py:40
  308.8 38.8 %fusion.2 = (bf16[2048,3072]{1,0:T(8,128)(2,1)}, f32[2048,3072]{1,0:T(8,128)}) fusion(f32[2048,3072]{1,0:T(8,128)} %fusion.28, bf16[2048,3072]{1,0:T(8,128)(2,1)} %convolution_convert_fusion.2, bf16[1,1280,3072]{2,1,0:T(8,128)(2,1)} %all-gather.19.cloned.1.call-done, bf16[2048,1280]{0,1:T(8,128)(2,1)} %get-tuple-element.27, f32[2048]{0:T(1024)S(1)} %fusion.91), kind=kOutput, calls=%fused_computation.8 | convolution fusion | flops 16189489152 | bytes 88612864 | tf_op jit(solution)/shard_map/jvp()/dot_general | solution.py:21
  347.7 22.6 %fusion.46 = bf16[2048,1280]{0,1:T(8,128)(2,1)} fusion(bf16[2048,3072]{1,0:T(8,128)(2,1)} %get-tuple-element.28, bf16[1,1280,3072]{2,1,0:T(8,128)(2,1)} %all-gather.19.cloned.1.call-done), kind=kOutput, calls=%fused_computation.62 | convolution fusion | flops 16106127360 | bytes 25690112 | tf_op jit(solution)/shard_map/transpose(jvp())/dot_general | solution.py:21
  370.3 28.0 %fusion.27 = (f32[2048]{0:T(1024)S(1)}, bf16[2048,1280]{0,1:T(8,128)(2,1)}) fusion(bf16[2048,1280]{0,1:T(8,128)(2,1)S(1)} %copy-done, bf16[2048,1280]{0,1:T(8,128)(2,1)} %fusion.46, bf16[1,1280,3072]{2,1,0:T(8,128)(2,1)} %all-gather.23.cloned.1.call-done, bf16[2048,3072]{1,0:T(8,128)(2,1)} %convolution_convert_fusion.2, f32[2048,3072]{1,0:T(8,128)} %get-tuple-element.29), kind=kOutput, calls=%fused_computation.45 | convolution fusion | flops 16159602688 | bytes 61349888 | tf_op jit(solution)/shard_map/transpose(jvp())/dot_general | solution.py:22
  398.3 12.3 %fusion.58 = bf16[2048,1280]{0,1:T(8,128)(2,1)} fusion(bf16[2048,1280]{0,1:T(8,128)(2,1)} %get-tuple-element.27, bf16[2048,1280]{0,1:T(8,128)(2,1)} %get-tuple-element.31, bf16[1,2048,1280]{1,2,0:T(8,128)(2,1)} %copy.21, f32[2048]{0:T(1024)S(1)} %multiply_multiply_fusion.3, f32[2048]{0:T(1024)S(1)} %fusion.91), kind=kLoop, calls=%fused_computation.66 | loop fusion | flops 18350080 | bytes 20987904 | tf_op jit(solution)/shard_map/transpose(jvp())/add_any | solution.py:14
  410.7 22.7 %convolution_convert_fusion = bf16[3072,1280]{1,0:T(8,128)(2,1)} fusion(bf16[2048,3072]{1,0:T(8,128)(2,1)} %get-tuple-element.24, bf16[2048,1280]{0,1:T(8,128)(2,1)} %fusion.58), kind=kOutput, calls=%fused_computation.31 | convolution fusion | flops 16110059520 | bytes 25690112 | tf_op jit(solution)/shard_map/transpose(jvp())/dot_general | solution.py:10
  433.4 0.0 reduce-scatter.15.cloned.1.call-update
  433.4 0.0 reduce-scatter.17.cloned.1.call-start
  433.5 28.4 %fusion.15 = bf16[3072,1280]{1,0:T(8,128)(2,1)} fusion(f32[2048,3072]{1,0:T(8,128)} %fusion.28, bf16[1,2048,1280]{2,1,0:T(8,128)(2,1)} %param.12, f32[2048,3072]{1,0:T(8,128)} %get-tuple-element.29), kind=kOutput, calls=%fused_computation.32 | convolution fusion | flops 16147808256 | bytes 63438848 | tf_op jit(solution)/shard_map/transpose(jvp())/dot_general | solution.py:10
  461.8 0.0 reduce-scatter.17.cloned.1.call-update
  461.9 0.0 reduce-scatter.11.cloned.1.call-start
  461.9 22.7 %convolution_convert_fusion.1 = bf16[2048,3072]{1,0:T(8,128)(2,1)} fusion(bf16[2048,1280]{0,1:T(8,128)(2,1)} %fusion.58, bf16[1,3072,1280]{2,1,0:T(8,128)(2,1)} %all-gather.17.cloned.1.call-done), kind=kOutput, calls=%fused_computation.35 | convolution fusion | flops 16112418816 | bytes 25690112 | tf_op jit(solution)/shard_map/transpose(jvp())/dot_general | solution.py:10
  484.6 25.0 %fusion.17 = bf16[1280,3072]{1,0:T(8,128)(2,1)} fusion(bf16[2048,3072]{1,0:T(8,128)(2,1)} %convolution_convert_fusion.1, f32[2048,3072]{1,0:T(8,128)} %fusion.41, bf16[1,2048,1280]{1,2,0:T(8,128)(2,1)} %copy.20, f32[2048]{0:T(1024)S(1)} %copy-done.17), kind=kOutput, calls=%fused_computation.34 | convolution fusion | flops 16155672576 | bytes 50864128 | tf_op jit(solution)/shard_map/transpose(jvp())/dot_general | solution.py:22
  509.6 0.0 reduce-scatter.13.cloned.1.call-start
  509.7 0.6 copy-done.13
  510.3 25.2 %fusion.16 = bf16[1280,3072]{1,0:T(8,128)(2,1)} fusion(bf16[2048,3072]{1,0:T(8,128)(2,1)} %convolution_convert_fusion.2, bf16[2048,1280]{0,1:T(8,128)(2,1)} %get-tuple-element.27, f32[2048]{0:T(1024)S(1)} %copy-done.13, f32[2048,3072]{1,0:T(8,128)} %get-tuple-element.29), kind=kOutput, calls=%fused_computation.33 | convolution fusion | flops 16155672576 | bytes 50864128 | tf_op jit(solution)/shard_map/transpose(jvp())/dot_general | solution.py:22
  535.6 0.0 reduce-scatter.7.cloned.1.call-start
  535.6 32.3 %fusion.18 = bf16[1280,3072]{1,0:T(8,128)(2,1)} fusion(f32[2048,3072]{1,0:T(8,128)} %fusion.41, f32[2048,3072]{1,0:T(8,128)} %get-tuple-element.25, bf16[2048,3072]{1,0:T(8,128)(2,1)} %convolution_convert_fusion.1, bf16[1,2048,1280]{1,2,0:T(8,128)(2,1)} %copy.20, f32[2048]{0:T(1024)S(1)} %copy-done.17), kind=kOutput, calls=%fused_computation.37 | convolution fusion | flops 16187129856 | bytes 76029952 | tf_op jit(solution)/shard_map/transpose(jvp())/dot_general | solution.py:21
  567.9 0.0 reduce-scatter.9.cloned.1.call-start
  567.9 22.4 %convolution_convert_fusion.3 = bf16[1280,3072]{1,0:T(8,128)(2,1)} fusion(bf16[2048,3072]{1,0:T(8,128)(2,1)} %get-tuple-element.28, bf16[2048,1280]{0,1:T(8,128)(2,1)} %get-tuple-element.27, f32[2048]{0:T(1024)S(1)} %copy-done.13), kind=kOutput, calls=%fused_computation.38 | convolution fusion | flops 16113991680 | bytes 25698304 | tf_op jit(solution)/shard_map/transpose(jvp())/dot_general | solution.py:21
  590.4 0.0 reduce-scatter.15.cloned.1.call-done
  590.5 0.0 reduce-scatter.17.cloned.1.call-done
  590.5 2.4 fusion.81
  592.9 68.6 %reduce-scatter.11.cloned.1.call-done = bf16[80,3072]{1,0:T(8,128)(2,1)} async-done(((bf16[1280,3072]{1,0:T(8,128)(2,1)}), bf16[80,3072]{1,0:T(8,128)(2,1)}) %reduce-scatter.11.cloned.1.call-update) | async-done | bytes 491536 | tf_op jit(solution)/shard_map/reduce_scatter | solution.py:53
  661.5 77.3 %reduce-scatter.13.cloned.1.call-done = bf16[80,3072]{1,0:T(8,128)(2,1)} async-done(((bf16[1280,3072]{1,0:T(8,128)(2,1)}), bf16[80,3072]{1,0:T(8,128)(2,1)}) %reduce-scatter.13.cloned.1.call-update) | async-done | bytes 491536 | tf_op jit(solution)/shard_map/reduce_scatter | solution.py:53
  738.8 2.3 fusion.80
  741.1 75.2 %reduce-scatter.7.cloned.1.call-done = bf16[80,3072]{1,0:T(8,128)(2,1)} async-done(((bf16[1280,3072]{1,0:T(8,128)(2,1)}), bf16[80,3072]{1,0:T(8,128)(2,1)}) %reduce-scatter.7.cloned.1.call-update) | async-done | bytes 491536 | tf_op jit(solution)/shard_map/reduce_scatter | solution.py:53
  816.2 77.3 %reduce-scatter.9.cloned.1.call-done = bf16[80,3072]{1,0:T(8,128)(2,1)} async-done(((bf16[1280,3072]{1,0:T(8,128)(2,1)}), bf16[80,3072]{1,0:T(8,128)(2,1)}) %reduce-scatter.9.cloned.1.call-update) | async-done | bytes 491536 | tf_op jit(solution)/shard_map/reduce_scatter | solution.py:53
  893.5 2.3 fusion.79
  897.8 31.8 %psum.7 = f32[]{:T(128)} all-reduce(f32[]{:T(128)S(6)} %add.99), channel_id=1, replica_groups=mesh['rep'=1,'dp'=16] {'dp'}, use_global_device_ids=true, to_apply=%region_12.13 | all-reduce | flops 1 | bytes 8 | tf_op jit(solution)/shard_map/psum | solution.py:55
  930.4 5.5 fusion.87
  936.0 0.4 copy-done.10
  936.4 0.9 copy-done.11
  937.3 4.9 fusion.78
  (39 shorter events, 0.2 us)
Async XLA Ops:
  7.2 53.4 %all-gather.13.cloned.1.call-start = ((), (), s32[]{:S(2)}) async-start(), calls=%async_computation.12 | async-start | bytes 8355840 | tf_op jit(solution)/shard_map/all_gather | solution.py:40
  9.4 100.9 %all-gather.15.cloned.1.call-start = ((), (), s32[]{:S(2)}) async-start(), calls=%async_computation.13 | async-start | bytes 8355840 | tf_op jit(solution)/shard_map/all_gather | solution.py:40
  11.7 148.4 %all-gather.17.cloned.1.call-start = ((), (), s32[]{:S(2)}) async-start(), calls=%async_computation.14 | async-start | bytes 8355840 | tf_op jit(solution)/shard_map/all_gather | solution.py:40
  13.9 195.7 %all-gather.21.cloned.1.call-start = ((), (), s32[]{:S(2)}) async-start(), calls=%async_computation.16 | async-start | bytes 8355840 | tf_op jit(solution)/shard_map/all_gather | solution.py:40
  14.5 244.7 %all-gather.23.cloned.1.call-start = ((), (), s32[]{:S(2)}) async-start(), calls=%async_computation.17 | async-start | bytes 8355840 | tf_op jit(solution)/shard_map/all_gather | solution.py:40
  15.1 293.7 %all-gather.19.cloned.1.call-start = ((), (), s32[]{:S(2)}) async-start(), calls=%async_computation.15 | async-start | bytes 8355840 | tf_op jit(solution)/shard_map/all_gather | solution.py:40
  15.7 574.8 %reduce-scatter.15.cloned.1.call-start = ((), (), s32[]{:S(2)}) async-start(), calls=%async_computation.10 | async-start | bytes 8355840 | tf_op jit(solution)/shard_map/reduce_scatter | solution.py:53
  27.3 83.0 %copy-start.16 = (f32[2048]{0:T(1024)}, f32[2048]{0:T(1024)S(1)}, u32[]{:S(2)}) copy-start(f32[2048]{0:T(1024)S(1)} %add_rsqrt_fusion) | copy-start | bytes 24580
  183.7 0.6 copy-start.14
  184.3 214.0 %copy-start.12 = (f32[2048]{0:T(1024)}, f32[2048]{0:T(1024)S(1)}, u32[]{:S(2)}) copy-start(f32[2048]{0:T(1024)S(1)} %fusion.91) | copy-start | bytes 24580
  347.7 22.6 %copy-start = (bf16[2048,1280]{0,1:T(8,128)(2,1)S(1)}, bf16[2048,1280]{0,1:T(8,128)(2,1)}, u32[]{:S(2)}) copy-start(bf16[2048,1280]{0,1:T(8,128)(2,1)} %get-tuple-element.27) | copy-start | bytes 15728644
  370.3 28.0 %copy-start.15 = (f32[2048]{0:T(1024)S(1)}, f32[2048]{0:T(1024)}, u32[]{:S(2)}) copy-start(f32[2048]{0:T(1024)} %copy-done.14) | copy-start | bytes 24580
  433.4 157.0 %reduce-scatter.17.cloned.1.call-start = ((), (), s32[]{:S(2)}) async-start(), calls=%async_computation.11 | async-start | bytes 8355840 | tf_op jit(solution)/shard_map/reduce_scatter | solution.py:53
  461.9 22.8 %copy-start.17 = (f32[2048]{0:T(1024)S(1)}, f32[2048]{0:T(1024)}, u32[]{:S(2)}) copy-start(f32[2048]{0:T(1024)} %copy-done.16) | copy-start | bytes 24580
  461.9 199.6 %reduce-scatter.11.cloned.1.call-start = ((), (), s32[]{:S(2)}) async-start(), calls=%async_computation.8 | async-start | bytes 8355840 | tf_op jit(solution)/shard_map/reduce_scatter | solution.py:53
  509.6 0.7 copy-start.13
  509.6 229.2 %reduce-scatter.13.cloned.1.call-start = ((), (), s32[]{:S(2)}) async-start(), calls=%async_computation.9 | async-start | bytes 8355840 | tf_op jit(solution)/shard_map/reduce_scatter | solution.py:53
  535.6 280.7 %reduce-scatter.7.cloned.1.call-start = ((), (), s32[]{:S(2)}) async-start(), calls=%async_computation.6 | async-start | bytes 8355840 | tf_op jit(solution)/shard_map/reduce_scatter | solution.py:53
  567.9 325.6 %reduce-scatter.9.cloned.1.call-start = ((), (), s32[]{:S(2)}) async-start(), calls=%async_computation.7 | async-start | bytes 8355840 | tf_op jit(solution)/shard_map/reduce_scatter | solution.py:53
  590.4 339.9 %copy-start.3 = (bf16[2,192,1280]{2,1,0:T(8,128)(2,1)S(1)}, bf16[2,192,1280]{2,1,0:T(8,128)(2,1)}, u32[]{:S(2)}) copy-start(bf16[2,192,1280]{2,1,0:T(8,128)(2,1)} %param.15) | copy-start | bytes 2949124
  590.4 345.5 %copy-start.1 = (bf16[2,80,3072]{2,1,0:T(8,128)(2,1)S(1)}, bf16[2,80,3072]{2,1,0:T(8,128)(2,1)}, u32[]{:S(2)}) copy-start(bf16[2,80,3072]{2,1,0:T(8,128)(2,1)} %param.13) | copy-start | bytes 2949124
  590.4 345.5 %copy-start.2 = (bf16[2,80,3072]{2,1,0:T(8,128)(2,1)S(1)}, bf16[2,80,3072]{2,1,0:T(8,128)(2,1)}, u32[]{:S(2)}) copy-start(bf16[2,80,3072]{2,1,0:T(8,128)(2,1)} %param.14) | copy-start | bytes 2949124
  661.5 274.4 %copy-start.4 = (bf16[80,3072]{1,0:T(8,128)(2,1)S(1)}, bf16[80,3072]{1,0:T(8,128)(2,1)}, u32[]{:S(2)}) copy-start(bf16[80,3072]{1,0:T(8,128)(2,1)} %reduce-scatter.11.cloned.1.call-done) | copy-start | bytes 1474564
  930.3 5.6 copy-start.5
  930.3 5.6 copy-start.6
  930.3 5.6 copy-start.7
  930.3 5.6 copy-start.8
  930.4 5.6 copy-start.9
  930.4 6.0 copy-start.10
  930.4 6.9 copy-start.11
Sparse Core Ops, SparseCore 0:
  10.8 49.7 all-gather.12
  63.4 46.8 all-gather.14
  113.1 46.8 all-gather.16
  162.7 46.8 all-gather.20
  212.3 46.8 all-gather.22
  261.9 46.8 all-gather.18
  433.6 73.0 reduce-scatter.14
  511.0 72.9 reduce-scatter.16
  588.5 72.9 reduce-scatter.10
  665.8 72.9 reduce-scatter.12
  743.2 72.9 reduce-scatter.6
  820.5 72.9 reduce-scatter.8
where the time goes:
time: 955 us; the launch traced here: 949 us
  waiting for transfers between devices  445 us (47%)
  matrix products  396 us (41%)
  other arithmetic  33.3 us (3%)
  blocking collectives  31.8 us (3%)
  local copies, waits for them, and re-layouts  25.1 us (3%)
  between operations  17.5 us (2%)
    reduce_scatter x6, waiting for transfers between devices, step(): lax.psum_scatter(by_w[name], 'dp', scatter_dimension=0, tiled=True)  298 us
    all_gather x6, waiting for transfers between devices, fetched(): lax.all_gather(w[number], 'dp', axis=0, tiled=True)  145 us
    dot_general x5, matrix products, layer(): gate = jnp.dot(a, w['w_gate'], preferred_element_type=jnp.float32)  140 us
    dot_general x5, matrix products, layer(): up = jnp.dot(a, w['w_up'], preferred_element_type=jnp.float32)  136 us
    dot_general x5, matrix products, matmul(): jnp.dot(a, w, preferred_element_type=jnp.float32).astype(jnp.bfloat16)  120 us
    psum x1, blocking collectives, step(): squares = lax.psum(sum((jnp.sum(g * g) for g in gradients)), 'dp')  31.8 us
  transfers between devices with their start and end apart: 12, of which 10 were waited for; matrix products, arithmetic and copies ran while one was open for 33% of the time, Pallas kernels for 0%

commit v1 on v0

v1 whole, which is shorter than its diff:
```python
import functools

import jax
import jax.numpy as jnp
from jax import lax
from jax.experimental import pallas as pl
from jax.experimental.pallas import tpu as pltpu
from jax.sharding import PartitionSpec as P

MESH = pl.DeviceIdType.MESH
F32, BF16 = jnp.float32, jnp.bfloat16
ANY = pl.BlockSpec(memory_space=pl.ANY)
AXES = (8, 4, 2)
TURNS = ((8, 4, 2), (4, 2, 8), (2, 8, 4))
TOKENS, D, FF = 2048, 1280, 3072
TILE = 256


class Here:
    def __init__(self):
        me = lax.axis_index("dp")
        self.me = me
        self.bit = {b: lax.rem(lax.div(me, b), 2) for b in (8, 4, 2, 1)}

    def peer(self, b):
        return {"dp": self.me + b * (1 - 2 * self.bit[b])}

    def at(self, how):
        out = []
        for b, h in how:
            out.append(self.bit[b] if h == "m" else 1 - self.bit[b] if h == "o" else slice(None))
        return tuple(out)


def send(src, dst, sems, i, device):
    return pltpu.make_async_remote_copy(
        src_ref=src, dst_ref=dst, send_sem=sems.at[0, i], recv_sem=sems.at[1, i], device_id=device, device_id_type=MESH
    )


def pieces(rows, cols):
    if cols == FF:
        third, half = FF // 3, FF // 6
        return [[(slice(0, rows), slice(r * third + h * half, r * third + (h + 1) * half)) for r in range(3)] for h in range(2)]
    third, half = rows // 3, cols // 2
    return [[(slice(r * third, (r + 1) * third), slice(h * half, (h + 1) * half)) for r in range(3)] for h in range(2)]


class Gather:
    peers = (8, 4, 2, 1)
    n_in = n_out = 1

    def __init__(self, blocks, layer, lag=0.0):
        self.array = blocks
        self.rows, self.cols = blocks.shape[1:]
        self.layer, self.lag = layer, lag

    def inputs(self):
        layer = self.layer
        return [(self.array, pl.BlockSpec((1, self.rows, self.cols), lambda *_: (layer, 0, 0)))]

    def outputs(self):
        return [(jax.ShapeDtypeStruct((2, 2, 2, 2, self.rows, self.cols), BF16), ANY)]

    def scratch(self):
        return [pltpu.SemaphoreType.DMA((2, 18)), pltpu.SemaphoreType.DMA((2, 19)), pltpu.SemaphoreType.DMA]

    def events(self, here, ins, outs, scratch):
        (own,), (full,), (wire, cores, local) = ins, outs, scratch
        own = own.at[0]
        parts = pieces(self.rows, self.cols)
        mine = here.at([(b, "m") for b in (8, 4, 2, 1)])

        def view(how, h, r):
            return full.at[here.at([(b, how.get(b, "m")) for b in (8, 4, 2, 1)]) + parts[h][r]]

        def hop(p, h, r):
            d = TURNS[r]
            src = view({b: "f" for b in d[:p]}, h, r)
            dst = src
            if p == 0:
                src = own.at[parts[h][r]]
            return send(src, dst, wire, (p * 2 + h) * 3 + r, here.peer(d[p]))

        def across(p, h, r):
            d = TURNS[r]
            ref = view({**{b: "f" for b in d[:p]}, d[p]: "o"}, h, r)
            return send(ref, ref, cores, (p * 2 + h) * 3 + r, here.peer(1))

        def own_across():
            return send(own, full.at[mine], cores, 18, here.peer(1))

        keep = pltpu.make_async_copy(own, full.at[mine], local)

        def begin():
            for h in range(2):
                for r in range(3):
                    hop(0, h, r).start()
            keep.start()
            own_across().start()
            keep.wait()

        def onward(p, h):
            for r in range(3):
                hop(p, h, r).wait_recv()
                if p < 2:
                    hop(p + 1, h, r).start()
                across(p, h, r).start()

        def finish():
            for p in range(3):
                for h in range(2):
                    for r in range(3):
                        hop(p, h, r).wait_send()
                        across(p, h, r).wait()
            own_across().wait()

        times = {(0, 0): 4.0, (0, 1): 5.8, (1, 0): 9.5, (1, 1): 13.0, (2, 0): 20.0, (2, 1): 27.0}
        out = [(self.lag, begin)]
        for (p, h), t in times.items():
            out.append((self.lag + t, functools.partial(onward, p, h)))
        out.append((1e9, finish))
        return out


class Scatter:
    peers = (8, 4, 2)
    n_in = n_out = 1

    def __init__(self, sums, lag=0.0):
        self.array = sums
        self.rows, self.cols = sums.shape[3:]
        self.lag = lag

    def inputs(self):
        return [(self.array, ANY)]

    def outputs(self):
        return [(jax.ShapeDtypeStruct((self.rows, self.cols), BF16), pl.BlockSpec((self.rows, self.cols), lambda *_: (0, 0)))]

    def scratch(self):
        r, c = pieces(self.rows, self.cols)[0][0]
        r, c = r.stop - r.start, c.stop - c.start
        legs = [pltpu.VMEM((6, *lead, r, c), BF16) for lead in ((2, 2), (2,), ())]
        return [pltpu.VMEM((2, 2, 2, self.rows, self.cols), F32), *legs, *legs, pltpu.SemaphoreType.DMA((2, 18)), pltpu.SemaphoreType.DMA]

    def events(self, here, ins, outs, scratch):
        (sums,), (out,) = ins, outs
        held, *legs, wire, local = scratch
        going, coming = legs[:3], legs[3:]
        parts = pieces(self.rows, self.cols)
        load = pltpu.make_async_copy(sums, held, local)

        def place(order, picks):
            where = dict(zip(order, picks, strict=True))
            return tuple(where[b] for b in AXES)

        def hop(p, h, r):
            q = h * 3 + r
            return send(going[p].at[q], coming[p].at[q], wire, p * 6 + q, here.peer(TURNS[r][p]))

        def begin():
            load.start()

        def first(h):
            if h == 0:
                load.wait()
            for r in range(3):
                d, q = TURNS[r], h * 3 + r
                for i in range(2):
                    for j in range(2):
                        going[0][q, i, j] = held[place(d, (1 - here.bit[d[0]], i, j)) + parts[h][r]].astype(BF16)
                hop(0, h, r).start()

        def onward(p, h):
            for r in range(3):
                d, q = TURNS[r], h * 3 + r
                mine = [here.bit[b] for b in d]
                hop(p, h, r).wait_recv()
                if p == 0:
                    for j in range(2):
                        at = place(d, (mine[0], 1 - mine[1], j)) + parts[h][r]
                        going[1][q, j] = (held[at] + coming[0][q, 1 - mine[1], j].astype(F32)).astype(BF16)
                    hop(1, h, r).start()
                    for j in range(2):
                        at = place(d, (mine[0], mine[1], j)) + parts[h][r]
                        held[at] = held[at] + coming[0][q, mine[1], j].astype(F32)
                elif p == 1:
                    at = place(d, (mine[0], mine[1], 1 - mine[2])) + parts[h][r]
                    going[2][q] = (held[at] + coming[1][q, 1 - mine[2]].astype(F32)).astype(BF16)
                    hop(2, h, r).start()
                    at = place(d, mine) + parts[h][r]
                    held[at] = held[at] + coming[1][q, mine[2]].astype(F32)
                else:
                    at = place(d, mine) + parts[h][r]
                    out[parts[h][r]] = (held[at] + coming[2][q].astype(F32)).astype(BF16)

        def finish():
            for p in range(3):
                for h in range(2):
                    for r in range(3):
                        hop(p, h, r).wait_send()

        times = {(0, 0): 11.0, (0, 1): 18.0, (1, 0): 22.0, (1, 1): 25.5, (2, 0): 27.5, (2, 1): 29.0}
        out_events = [(self.lag, begin), (self.lag + 2.5, functools.partial(first, 0)), (self.lag + 3.0, functools.partial(first, 1))]
        for (p, h), t in times.items():
            out_events.append((self.lag + t, functools.partial(onward, p, h)))
        out_events.append((1e9, finish))
        return out_events


class Total:
    peers = "all"
    n_out = 1

    def __init__(self, blocks):
        self.blocks = blocks
        self.n_in = len(blocks)

    def inputs(self):
        return [(b, pl.BlockSpec(b.shape, lambda *_: (0, 0))) for b in self.blocks]

    def outputs(self):
        return [(jax.ShapeDtypeStruct((8, 128), F32), pl.BlockSpec((8, 128), lambda *_: (0, 0)))]

    def scratch(self):
        return [pltpu.VMEM((16, 8, 128), F32), pltpu.SemaphoreType.DMA((2, 16))]

    def run(self, here, ins, outs, scratch, last):
        (all_sums, sems), (out,) = scratch, outs

        def squares(ref):
            rows, cols = ref.shape

            def step(i, acc):
                g = ref[pl.ds(pl.multiple_of(i * 16, 16), 16), :].astype(F32)
                g = g * g
                return acc + sum(g[:, k * 128 : (k + 1) * 128] for k in range(cols // 128))

            s = lax.fori_loop(0, rows // 16, step, jnp.zeros((16, 128), F32))
            return s[:8] + s[8:]

        total = sum(squares(ref) for ref in (*ins, last))
        all_sums[here.me] = total
        copies = []
        for k in range(1, 16):
            to = lax.rem(here.me + k, 16)
            copies.append(send(all_sums.at[here.me], all_sums.at[here.me], sems, k, {"dp": to}))
        for c in copies:
            c.start()
        for c in copies:
            c.wait()
        total = all_sums[0]
        for k in range(1, 16):
            total = total + all_sums[k]
        out[...] = jnp.full((8, 128), jnp.sum(total), F32)


def stage(cid, name, steps, step_us, body, ins, outs, scratch=(), own_peers=(), comms=(), total=None, flops=0):
    comms = list(comms)
    everyone = comms + ([total] if total else [])
    args = [*ins] + [x for c in everyone for x in c.inputs()]
    results = [*outs] + [x for c in everyone for x in c.outputs()]
    temps = [*scratch] + [x for c in everyone for x in c.scratch()]
    peers = sorted({b for c in comms for b in c.peers} | set(own_peers))

    def kernel(*refs):
        here = Here()
        i, o = refs[: len(args)], refs[len(args) : len(args) + len(results)]
        s = refs[len(args) + len(results) :]
        at = pl.program_id(0)

        def barrier():
            sem = pltpu.get_barrier_semaphore()
            if total:
                for k in range(1, 16):
                    pl.semaphore_signal(sem, inc=1, device_id={"dp": lax.rem(here.me + k, 16)}, device_id_type=MESH)
                pl.semaphore_wait(sem, 15)
            else:
                for b in peers:
                    pl.semaphore_signal(sem, inc=1, device_id=here.peer(b), device_id_type=MESH)
                pl.semaphore_wait(sem, len(peers))

        events, ni, no, ns = [], len(ins), len(outs), len(scratch)
        for c in comms:
            ci, co, cs = i[ni : ni + c.n_in], o[no : no + c.n_out], s[ns : ns + len(c.scratch())]
            ni, no, ns = ni + c.n_in, no + c.n_out, ns + len(c.scratch())
            events += c.events(here, ci, co, cs)
        events.sort(key=lambda e: e[0])
        by_step = {}
        for t, fn in events:
            by_step.setdefault(min(steps, int(t / step_us)) if t < 1e9 else steps + 1, []).append(fn)

        def run(fns):
            for fn in fns:
                fn()

        @pl.when(at == 0)
        def _():
            if peers or total:
                barrier()
            run(by_step.get(0, []))

        for k in range(1, steps):
            if k in by_step:
                pl.when(at == k)(functools.partial(run, by_step[k]))
        if body:
            body(here, at, i[: len(ins)], o[: len(outs)], s[: len(scratch)])

        @pl.when(at == steps - 1)
        def _():
            run(by_step.get(steps, []) + by_step.get(steps + 1, []))
            if total:
                total.run(here, i[ni:], o[no:], s[ns:], o[no - 1])

    got = pl.pallas_call(
        kernel,
        grid=(steps,),
        in_specs=[spec for _, spec in args],
        out_specs=[spec for _, spec in results],
        out_shape=[shape for shape, _ in results],
        scratch_shapes=temps,
        compiler_params=pltpu.CompilerParams(
            collective_id=cid if (peers or total) else None, has_side_effects=bool(peers or total), vmem_limit_bytes=63 * 1024 * 1024
        ),
        name=name,
    )(*[a for a, _ in args])
    return got


def whole(array):
    return (array, pl.BlockSpec(array.shape, lambda *_: (0,) * array.ndim, pipeline_mode=pl.Buffered(1)))


def by_cols(array, width=TILE, last=None):
    lead = array.shape[:-1]
    return (array, pl.BlockSpec((*lead, width), lambda i: (0,) * len(lead) + (i if last is None else jnp.minimum(i, last),)))


def by_rows(array, height):
    return (array, pl.BlockSpec((height, array.shape[1]), lambda i: (i, 0)))


def new(shape, dtype, block, index):
    return (jax.ShapeDtypeStruct(shape, dtype), pl.BlockSpec(block, index))


def mm(a, b):
    return lax.dot_general(a, b, (((1,), (0,)), ((), ())), preferred_element_type=F32)


def mm_nt(a, b):
    return lax.dot_general(a, b, (((1,), (1,)), ((), ())), preferred_element_type=F32)


def chunks(total, size, fn):
    def step(i, _):
        fn(pl.ds(pl.multiple_of(i * size, size), size))
        return 0

    lax.fori_loop(0, total // size, step, 0)


def norm_of(wide):
    scale = lax.rsqrt(jnp.mean(wide * wide, -1, keepdims=True) + 1e-6)
    return (wide * scale).astype(BF16)


COL = lambda i: (0, i)
ROW = lambda i: (i, 0)


def norm_stage(cid, x, comms):
    def body(here, at, ins, outs, scratch):
        a = norm_of(ins[0][...].astype(F32))
        outs[0][...] = a
        outs[1][...] = a.T

    outs = [new((TOKENS, D), BF16, (256, D), ROW), new((D, TOKENS), BF16, (D, 256), COL)]
    return stage(cid, "norm", 8, 1.0, body, [by_rows(x, 256)], outs, comms=comms)


def gate_up_stage(cid, a, wg, wu, comms):
    def body(here, at, ins, outs, scratch):
        a, wg, wu = ins
        g_out, u_out, act_out, act_t = outs

        def part(rows):
            g = mm(a[rows, :], wg[...])
            u = mm(a[rows, :], wu[...])
            act = (g * jax.nn.sigmoid(g) * u).astype(BF16)
            g_out[rows, :] = g
            u_out[rows, :] = u
            act_out[rows, :] = act
            act_t[:, rows] = act.T

        chunks(TOKENS, 512, part)

    tile = (TOKENS, TILE)
    outs = [new((TOKENS, FF), t, tile, COL) for t in (F32, F32, BF16)] + [new((FF, TOKENS), BF16, (TILE, TOKENS), ROW)]
    return stage(cid, "gate_up", FF // TILE, 2.8, body, [whole(a), by_cols(wg), by_cols(wu)], outs, comms=comms)


def gate_stage(cid, a, wg, comms):
    def body(here, at, ins, outs, scratch):
        def part(rows):
            outs[0][rows, :] = mm(ins[0][rows, :], ins[1][...])

        chunks(TOKENS, 512, part)

    outs = [new((TOKENS, FF), F32, (TOKENS, TILE), COL)]
    return stage(cid, "gate", FF // TILE, 1.5, body, [whole(a), by_cols(wg)], outs, comms=comms)


def up_stage(cid, a, wu, g, comms):
    def body(here, at, ins, outs, scratch):
        a, wu, g_in = ins
        u_out, act_t = outs

        def part(rows):
            u = mm(a[rows, :], wu[...])
            g = g_in[rows, :]
            act = (g * jax.nn.sigmoid(g) * u).astype(BF16)
            u_out[rows, :] = u
            act_t[:, rows] = act.T

        chunks(TOKENS, 512, part)

    outs = [new((TOKENS, FF), F32, (TOKENS, TILE), COL), new((FF, TOKENS), BF16, (TILE, TOKENS), ROW)]
    return stage(cid, "up", FF // TILE, 1.5, body, [whole(a), by_cols(wu), by_cols(g)], outs, comms=comms)


def down_stage(cid, act, wd, x, comms):
    def body(here, at, ins, outs, scratch):
        act, wd, x = ins

        def part(rows):
            y = mm(act[rows, :], wd[...]).astype(BF16)
            h = x[rows, :] + y
            outs[0][rows, :] = h
            a = norm_of(h.astype(F32))
            outs[1][rows, :] = a
            outs[2][:, rows] = a.T

        chunks(512, 256, part)

    outs = [new((TOKENS, D), BF16, (512, D), ROW), new((TOKENS, D), BF16, (512, D), ROW), new((D, TOKENS), BF16, (D, 512), COL)]
    return stage(cid, "down", 4, 4.3, body, [by_rows(act, 512), whole(wd), by_rows(x, 512)], outs, comms=comms)


def dact_stage(cid, dy, wd, g, u, comms):
    def body(here, at, ins, outs, scratch):
        dy, wd, g_in, u_in = ins

        def part(rows):
            dact = mm_nt(dy[rows, :], wd[...]).astype(BF16).astype(F32)
            g, u = g_in[rows, :], u_in[rows, :]
            s = jax.nn.sigmoid(g)
            silu = g * s
            outs[0][rows, :] = (dact * u * (s + silu * (1.0 - s))).astype(BF16)
            outs[1][rows, :] = (dact * silu).astype(BF16)

        chunks(TOKENS, 512, part)

    outs = [new((TOKENS, FF), BF16, (TOKENS, TILE), COL)] * 2
    ins = [whole(dy), (wd, pl.BlockSpec((TILE, D), ROW)), by_cols(g), by_cols(u)]
    return stage(cid, "dact", FF // TILE, 1.5, body, ins, outs, comms=comms)


def dinput_stage(cid, dg, du, wg, wu, h, dy, comms):
    def body(here, at, ins, outs, scratch):
        dg, du, wg, wu, h, dy = ins

        def part(rows):
            da = mm_nt(dg[rows, :], wg[...]).astype(BF16) + mm_nt(du[rows, :], wu[...]).astype(BF16)
            da = da.astype(F32)
            wide = h[rows, :].astype(F32)
            scale = lax.rsqrt(jnp.mean(wide * wide, -1, keepdims=True) + 1e-6)
            along = jnp.mean(da * wide, -1, keepdims=True)
            dh = da * scale - wide * (scale * scale * scale * along)
            outs[0][rows, :] = dy[rows, :] + dh.astype(BF16)

        chunks(512, 256, part)

    outs = [new((TOKENS, D), BF16, (512, D), ROW)]
    ins = [by_rows(dg, 512), by_rows(du, 512), whole(wg), whole(wu), by_rows(h, 512), by_rows(dy, 512)]
    return stage(cid, "dinput", 4, 8.5, body, ins, outs, comms=comms)


def dw_stage(cid, left, right, comms):
    m, n = left.shape[0], right.shape[1]
    rows, tiles = m // 16, n // TILE
    group = 4 if rows == 80 else 2

    def body(here, at, ins, outs, scratch):
        left, right = ins
        acc, going, coming, sems = scratch
        core = here.bit[1]

        def swap(t):
            return send(going.at[t], coming.at[t], sems, t, here.peer(1))

        @pl.when(at < tiles)
        def _():
            slot = lax.rem(at, 2)

            def part(k, _):
                span = group * 2 * rows
                got = mm(left[pl.ds(pl.multiple_of(k * span, 16), span), :], right[...])
                acc[slot, pl.ds(k * group, group)] = got.reshape(group, 2, rows, TILE)
                return 0

            lax.fori_loop(0, 8 // group, part, 0)

            def put(k, _):
                going[at, k] = acc[slot, k, 1 - core].astype(BF16)
                return 0

            lax.fori_loop(0, 8, put, 0)
            swap(at).start()

        @pl.when(at > 0)
        def _():
            t = at - 1
            slot = lax.rem(t, 2)
            swap(t).wait()
            for a in range(2):
                for b in range(2):
                    for c in range(2):
                        k = a * 4 + b * 2 + c
                        outs[0][a, b, c] = acc[slot, k, core] + coming[t, k].astype(F32)

    back = lambda i: (0, 0, 0, 0, jnp.maximum(i - 1, 0))
    outs = [new((2, 2, 2, rows, n), F32, (2, 2, 2, rows, TILE), back)]
    scratch = [
        pltpu.VMEM((2, 8, 2, rows, TILE), F32),
        pltpu.VMEM((tiles, 8, rows, TILE), BF16),
        pltpu.VMEM((tiles, 8, rows, TILE), BF16),
        pltpu.SemaphoreType.DMA((2, tiles)),
    ]
    ins = [whole(left), by_cols(right, last=tiles - 1)]
    return stage(cid, "dw", tiles + 1, 17.5 / tiles, body, ins, outs, scratch, own_peers=(1,), comms=comms)


def adamw(w, m, v, g):
    m = 0.9 * m + 0.1 * g
    v = 0.95 * v + 0.05 * g * g
    step = m * lax.rsqrt(v + 1e-8) + 0.1 * w
    return (w - 0.02 * step).astype(jnp.bfloat16), m, v


def clipped(gradients, sum_of_squares, count):
    factor = jnp.minimum(1.0, 0.5 * lax.rsqrt(sum_of_squares / count + 1e-30))
    return [g * factor for g in gradients]


def solution(mesh):
    def step(x, dy, *arrays):
        weights, m, v = (arrays[i : i + 3] for i in (0, 3, 6))
        wg, wu, wd = weights
        x, dy = x[0], dy[0]
        up2 = lambda w: w.reshape(D, FF)
        down2 = lambda w: w.reshape(FF, D)

        a0, a0_t, wg0, wu0 = norm_stage(0, x, [Gather(wg, 0), Gather(wu, 0, 0.5)])
        g0, u0, act0, act0_t, wd0 = gate_up_stage(1, a0, up2(wg0), up2(wu0), [Gather(wd, 0)])
        h1, a1, a1_t, wg1 = down_stage(2, act0, down2(wd0), x, [Gather(wg, 1)])
        g1, wu1 = gate_stage(3, a1, up2(wg1), [Gather(wu, 1)])
        u1, act1_t, wd1 = up_stage(4, a1, up2(wu1), g1, [Gather(wd, 1)])
        (s_d1,) = dw_stage(5, act1_t, dy, [])
        dg1, du1, r_d1 = dact_stage(6, dy, down2(wd1), g1, u1, [Scatter(s_d1)])
        (s_g1,) = dw_stage(7, a1_t, dg1, [])
        s_u1, r_g1 = dw_stage(8, a1_t, du1, [Scatter(s_g1)])
        dh1, r_u1 = dinput_stage(9, dg1, du1, up2(wg1), up2(wu1), h1, dy, [Scatter(s_u1)])
        dg0, du0 = dact_stage(10, dh1, down2(wd0), g0, u0, [])
        (s_d0,) = dw_stage(11, act0_t, dh1, [])
        s_g0, r_d0 = dw_stage(12, a0_t, dg0, [Scatter(s_d0)])
        s_u0, r_g0 = dw_stage(13, a0_t, du0, [Scatter(s_g0)])
        r_u0, squares = stage(14, "last", 1, 1.0, None, [], [], comms=[Scatter(s_u0)], total=Total([r_d1, r_g1, r_u1, r_d0, r_g0]))

        gradients = [jnp.stack(pair).astype(F32) for pair in ((r_g0, r_g1), (r_u0, r_u1), (r_d0, r_d1))]
        gradients = clipped(gradients, squares[0, 0], 16 * sum(g.size for g in gradients))
        new_ = [adamw(w.astype(F32), m, v, g) for w, m, v, g in zip(weights, m, v, gradients, strict=True)]
        return tuple(one[which] for which in range(3) for one in new_)

    states, cut = P(("rep", "dp"), None, None), P(None, "dp", None)
    return jax.shard_map(
        step,
        mesh=mesh,
        in_specs=(states, states) + (cut,) * 9,
        out_specs=(P("rep", "dp", None),) * 9,
        check_vma=False,
    )
```

time: 955 us -> 647 us (0.68)
  Pallas kernels: 0 us -> 631 us
  waiting for transfers between devices: 445 us -> 0 us
  matrix products: 396 us -> 0 us
  blocking collectives: 31.8 us -> 0 us
  local copies, waits for them, and re-layouts: 25.1 us -> 2.93 us
  other arithmetic: 33.3 us -> 11.4 us
  between operations: 17.5 us -> 1.54 us
    pallas_call x0 -> x15, Pallas kernels: none -> 631 us  [stage(): pl.pallas_call(kernel, grid=(steps,), in_specs=[spec for _, spec in args]...]
    dot_general x15 -> x0, matrix products: 396 us -> none  [the longest x5 140 us: layer(): gate = jnp.dot(a, w['w_gate'], preferred_element_type=jnp.float32)]
    reduce_scatter x6 -> x0, waiting for transfers between devices: 298 us -> none  [step(): lax.psum_scatter(by_w[name], 'dp', scatter_dimension=0, tiled=True)]
    all_gather x6 -> x0, waiting for transfers between devices: 145 us -> none  [fetched(): lax.all_gather(w[number], 'dp', axis=0, tiled=True)]
    psum x1 -> x0, blocking collectives: 31.8 us -> none  [step(): squares = lax.psum(sum((jnp.sum(g * g) for g in gradients)), 'dp')]
    unnamed x38 -> x18, local copies, waits for them, and re-layouts: 18.5 us -> 1.74 us
    add_any x1 -> x0, other arithmetic: 12.3 us -> none  [normed(): wide = h.astype(jnp.float32)]
    reduce_sum x4 -> x0, other arithmetic: 10.6 us -> none  [the longest x3 7.02 us: step(): squares = lax.psum(sum((jnp.sum(g * g) for g in gradients)), 'dp')]
  transfers between devices with their start and end apart: 12 -> 0, of which waited for: 10 -> 0; matrix products, arithmetic and copies ran while one was open for 33% -> 0% of each run, Pallas kernels for 0% -> 0%
where the time goes in v1:
time: 647 us; the launch traced here: 646 us
  Pallas kernels  631 us (98%)
  other arithmetic  11.4 us (2%)
    pallas_call x15, Pallas kernels, stage(): pl.pallas_call(kernel, grid=(steps,), in_specs=[spec for _, spec in args]...  631 us

profile of v1, /device:TPU:0, one launch (start us, length us, event | category | flops | bytes accessed | tf_op | source)
XLA Modules:
  0.0 646.4 jit_solution(17835463643038488832)
XLA Ops:
  0.6 60.5 %norm.1 = (bf16[2048,1280]{1,0:T(8,128)(2,1)}, bf16[1280,2048]{1,0:T(8,128)(2,1)}, bf16[2,2,2,2,80,3072]{5,4,3,2,1,0:T(8,128)(2,1)}, bf16[2,2,2,2,80,3072]{5,4,3,2,1,0:T(8,128)(2,1)}) custom-call(bf16[2048,1280]{1,0:T(8,128)(2,1)} %bitcast.24, bf16[2,80,3072]{2,1,0:T(8,128)(2,1)} %refs_3_.4, bf16[2,80,3072]{2,1,0:T(8,128)(2,1)} %refs_2_.3), custom_call_target="tpu_custom_call" | custom-call | tf_op jit(solution)/shard_map/norm/pallas_call | solution.py:316
  61.1 55.1 %gate_up.1 = (f32[2048,3072]{1,0:T(8,128)}, f32[2048,3072]{1,0:T(8,128)}, bf16[2048,3072]{1,0:T(8,128)(2,1)}, bf16[3072,2048]{1,0:T(8,128)(2,1)}, bf16[2,2,2,2,192,1280]{5,4,3,2,1,0:T(8,128)(2,1)}) custom-call(bf16[2048,1280]{1,0:T(8,128)(2,1)} %get-tuple-element.43.refs_0_, bf16[1280,3072]{1,0:T(8,128)(2,1)} %bitcast.27, bf16[1280,3072]{1,0:T(8,128)(2,1)} %bitcast.28, ...), custom_call_target="tpu_custom_call" | custom-call | tf_op jit(solution)/shard_map/gate_up/pallas_call | solution.py:316
  116.2 39.1 %down.1 = (bf16[2048,1280]{1,0:T(8,128)(2,1)}, bf16[2048,1280]{1,0:T(8,128)(2,1)}, bf16[1280,2048]{1,0:T(8,128)(2,1)}, bf16[2,2,2,2,80,3072]{5,4,3,2,1,0:T(8,128)(2,1)}) custom-call(bf16[2048,3072]{1,0:T(8,128)(2,1)} %get-tuple-element.46.refs_0_, bf16[3072,1280]{1,0:T(8,128)(2,1)} %bitcast.22, bf16[2048,1280]{1,0:T(8,128)(2,1)} %bitcast.25, ...), custom_call_target="tpu_custom_call" | custom-call | tf_op jit(solution)/shard_map/down/pallas_call | solution.py:316
  155.4 37.9 %gate.1 = (f32[2048,3072]{1,0:T(8,128)}, bf16[2,2,2,2,80,3072]{5,4,3,2,1,0:T(8,128)(2,1)}) custom-call(bf16[2048,1280]{1,0:T(8,128)(2,1)} %get-tuple-element.48.refs_0_, bf16[1280,3072]{1,0:T(8,128)(2,1)} %bitcast.20, bf16[2,80,3072]{2,1,0:T(8,128)(2,1)} %refs_2_.3), custom_call_target="tpu_custom_call" | custom-call | tf_op jit(solution)/shard_map/gate/pallas_call | solution.py:316
  193.2 42.5 %up.1 = (f32[2048,3072]{1,0:T(8,128)}, bf16[3072,2048]{1,0:T(8,128)(2,1)}, bf16[2,2,2,2,192,1280]{5,4,3,2,1,0:T(8,128)(2,1)}) custom-call(bf16[2048,1280]{1,0:T(8,128)(2,1)} %get-tuple-element.48.refs_0_, bf16[1280,3072]{1,0:T(8,128)(2,1)} %bitcast.18, f32[2048,3072]{1,0:T(8,128)} %get-tuple-element.51.refs_2_, bf16[2,192,1280]{2,1,0:T(8,128)(2,1)} %refs_3_.5), custom_call_target="tpu_custom_call" | custom-call | tf_op jit(solution)/shard_map/up/pallas_call | solution.py:316
  235.7 29.5 %dw.6.refs_4_ = f32[2,2,2,192,1280]{4,3,2,1,0:T(8,128)} custom-call(bf16[3072,2048]{1,0:T(8,128)(2,1)} %get-tuple-element.54.refs_0_, bf16[2048,1280]{1,0:T(8,128)(2,1)} %bitcast.15), custom_call_target="tpu_custom_call" | custom-call | tf_op jit(solution)/shard_map/dw/pallas_call | solution.py:316
  265.2 51.7 %dact.2 = (bf16[2048,3072]{1,0:T(8,128)(2,1)}, bf16[2048,3072]{1,0:T(8,128)(2,1)}, bf16[192,1280]{1,0:T(8,128)(2,1)}) custom-call(bf16[2048,1280]{1,0:T(8,128)(2,1)} %bitcast.16, bf16[3072,1280]{1,0:T(8,128)(2,1)} %bitcast.26, f32[2048,3072]{1,0:T(8,128)} %get-tuple-element.51.refs_2_, f32[2048,3072]{1,0:T(8,128)} %get-tuple-element.53.refs_3_, ...), custom_call_target="tpu_custom_call" | custom-call | tf_op jit(solution)/shard_map/dact/pallas_call | solution.py:316
  316.9 28.0 %dw.7.refs_2_ = f32[2,2,2,80,3072]{4,3,2,1,0:T(8,128)} custom-call(bf16[1280,2048]{1,0:T(8,128)(2,1)} %get-tuple-element.58.refs_0_, bf16[2048,3072]{1,0:T(8,128)(2,1)} %get-tuple-element.55.refs_1_.refs_0_), custom_call_target="tpu_custom_call" | custom-call | tf_op jit(solution)/shard_map/dw/pallas_call | solution.py:316
  344.9 40.2 %dw.8 = (f32[2,2,2,80,3072]{4,3,2,1,0:T(8,128)}, bf16[80,3072]{1,0:T(8,128)(2,1)}) custom-call(bf16[1280,2048]{1,0:T(8,128)(2,1)} %get-tuple-element.58.refs_0_, bf16[2048,3072]{1,0:T(8,128)(2,1)} %get-tuple-element.56.refs_1_, f32[2,2,2,80,3072]{4,3,2,1,0:T(8,128)} %dw.7.refs_2_), custom_call_target="tpu_custom_call" | custom-call | tf_op jit(solution)/shard_map/dw/pallas_call | solution.py:316
  385.2 56.8 %dinput.1 = (bf16[2048,1280]{1,0:T(8,128)(2,1)}, bf16[80,3072]{1,0:T(8,128)(2,1)}) custom-call(bf16[2048,3072]{1,0:T(8,128)(2,1)} %get-tuple-element.55.refs_1_.refs_0_, bf16[2048,3072]{1,0:T(8,128)(2,1)} %get-tuple-element.56.refs_1_, bf16[1280,3072]{1,0:T(8,128)(2,1)} %bitcast.21, bf16[1280,3072]{1,0:T(8,128)(2,1)} %bitcast.19, ...), custom_call_target="tpu_custom_call" | custom-call | tf_op jit(solution)/shard_map/dinput/pallas_call | solution.py:316
  442.0 39.7 %dact.3 = (bf16[2048,3072]{1,0:T(8,128)(2,1)}, bf16[2048,3072]{1,0:T(8,128)(2,1)}) custom-call(bf16[2048,1280]{1,0:T(8,128)(2,1)} %get-tuple-element.60.refs_0_.refs_1_, bf16[3072,1280]{1,0:T(8,128)(2,1)} %bitcast.23, f32[2048,3072]{1,0:T(8,128)} %get-tuple-element.61.refs_2_, f32[2048,3072]{1,0:T(8,128)} %get-tuple-element.62.refs_3_), custom_call_target="tpu_custom_call" | custom-call | tf_op jit(solution)/shard_map/dact/pallas_call | solution.py:316
  481.7 29.6 %dw.9.refs_2_ = f32[2,2,2,192,1280]{4,3,2,1,0:T(8,128)} custom-call(bf16[3072,2048]{1,0:T(8,128)(2,1)} %get-tuple-element.65.refs_0_, bf16[2048,1280]{1,0:T(8,128)(2,1)} %get-tuple-element.60.refs_0_.refs_1_), custom_call_target="tpu_custom_call" | custom-call | tf_op jit(solution)/shard_map/dw/pallas_call | solution.py:316
  511.2 40.0 %dw.10 = (f32[2,2,2,80,3072]{4,3,2,1,0:T(8,128)}, bf16[192,1280]{1,0:T(8,128)(2,1)}) custom-call(bf16[1280,2048]{1,0:T(8,128)(2,1)} %get-tuple-element.42.refs_0_, bf16[2048,3072]{1,0:T(8,128)(2,1)} %get-tuple-element.64.refs_1_, f32[2,2,2,192,1280]{4,3,2,1,0:T(8,128)} %dw.9.refs_2_), custom_call_target="tpu_custom_call" | custom-call | tf_op jit(solution)/shard_map/dw/pallas_call | solution.py:316
  551.3 40.0 %dw.11 = (f32[2,2,2,80,3072]{4,3,2,1,0:T(8,128)}, bf16[80,3072]{1,0:T(8,128)(2,1)}) custom-call(bf16[1280,2048]{1,0:T(8,128)(2,1)} %get-tuple-element.42.refs_0_, bf16[2048,3072]{1,0:T(8,128)(2,1)} %get-tuple-element.63.refs_1_, f32[2,2,2,80,3072]{4,3,2,1,0:T(8,128)} %get-tuple-element.66.refs_2_), custom_call_target="tpu_custom_call" | custom-call | tf_op jit(solution)/shard_map/dw/pallas_call | solution.py:316
  591.3 0.0 copy-start.2
  591.3 40.0 %last.1 = (bf16[80,3072]{1,0:T(8,128)(2,1)}, f32[8,128]{1,0:T(8,128)}) custom-call(f32[2,2,2,80,3072]{4,3,2,1,0:T(8,128)} %get-tuple-element.69.refs_0_, bf16[192,1280]{1,0:T(8,128)(2,1)} %get-tuple-element.70.refs_1_, bf16[80,3072]{1,0:T(8,128)(2,1)} %get-tuple-element.68.refs_2_, bf16[80,3072]{1,0:T(8,128)(2,1)} %get-tuple-element.71.refs_3_, ...), custom_call_target="tpu_custom_call" | custom-call | tf_op jit(solution)/shard_map/last/pallas_call | solution.py:316
  631.3 1.2 slice.3
  633.2 0.0 copy-done.2
  633.2 0.0 copy-start
  633.2 0.0 copy-start.1
  633.2 0.0 copy-start.3
  633.2 0.0 copy-start.4
  633.2 0.0 copy-start.5
  633.3 0.0 copy-start.6
  633.3 0.0 copy-start.7
  633.3 0.0 copy-start.8
  633.3 5.5 fusion.8
  638.8 0.0 copy-done
  638.8 0.0 copy-done.1
  638.8 0.0 copy-done.3
  638.8 0.0 copy-done.4
  638.8 0.9 copy-done.5
  639.7 0.6 copy-done.6
  640.3 0.0 copy-done.7
  640.4 0.1 copy-done.8
  640.5 5.9 fusion.2
Async XLA Ops:
  591.3 41.9 %copy-start.2 = (bf16[2,192,1280]{2,1,0:T(8,128)(2,1)S(1)}, bf16[2,192,1280]{2,1,0:T(8,128)(2,1)}, u32[]{:S(2)}) copy-start(bf16[2,192,1280]{2,1,0:T(8,128)(2,1)} %refs_3_.5) | copy-start | bytes 2949124
  633.2 5.6 copy-start
  633.2 5.6 copy-start.1
  633.2 5.6 copy-start.3
  633.2 5.6 copy-start.4
  633.2 6.5 %copy-start.5 = (f32[2,80,3072]{2,1,0:T(8,128)S(1)}, f32[2,80,3072]{2,1,0:T(8,128)}, u32[]{:S(2)}) copy-start(f32[2,80,3072]{2,1,0:T(8,128)} %param.20) | copy-start | bytes 5898244
  633.3 7.1 %copy-start.6 = (f32[2,80,3072]{2,1,0:T(8,128)S(1)}, f32[2,80,3072]{2,1,0:T(8,128)}, u32[]{:S(2)}) copy-start(f32[2,80,3072]{2,1,0:T(8,128)} %param.17) | copy-start | bytes 5898244
  633.3 7.1 %copy-start.7 = (bf16[80,3072]{1,0:T(8,128)(2,1)S(1)}, bf16[80,3072]{1,0:T(8,128)(2,1)}, u32[]{:S(2)}) copy-start(bf16[80,3072]{1,0:T(8,128)(2,1)} %get-tuple-element.68.refs_2_) | copy-start | bytes 1474564
  633.3 7.2 %copy-start.8 = (bf16[80,3072]{1,0:T(8,128)(2,1)S(1)}, bf16[80,3072]{1,0:T(8,128)(2,1)}, u32[]{:S(2)}) copy-start(bf16[80,3072]{1,0:T(8,128)(2,1)} %get-tuple-element.71.refs_3_) | copy-start | bytes 1474564

commit v2 on v0

v2 whole, which is shorter than its diff:
```python
import functools

import jax
import jax.numpy as jnp
from jax import lax
from jax.experimental import pallas as pl
from jax.experimental.pallas import tpu as pltpu
from jax.sharding import PartitionSpec as P

MESH = pl.DeviceIdType.MESH
F32, BF16 = jnp.float32, jnp.bfloat16
ANY = pl.BlockSpec(memory_space=pl.ANY)
BITS = (8, 4, 2, 1)
AXES = BITS[:3]
TURNS = ((8, 4, 2), (4, 2, 8), (2, 8, 4))
TOKENS, D, FF = 2048, 1280, 3072
NIL, SPAN = 0, 256
PAIR, THIRDS = range(2), range(3)


class Here:
    def __init__(self):
        me = lax.axis_index("dp")
        self.me = me
        self.bit = {b: lax.rem(lax.div(me, b), 2) for b in BITS}

    def peer(self, b):
        return {"dp": self.me + b * (1 - 2 * self.bit[b])}

    def at(self, how):
        out = []
        for b, h in how:
            out.append(self.bit[b] if h == "m" else 1 - self.bit[b] if h == "o" else slice(None))
        return tuple(out)


def send(src, dst, sems, i, device):
    return pltpu.make_async_remote_copy(
        src_ref=src, dst_ref=dst, send_sem=sems.at[NIL, i], recv_sem=sems.at[1, i], device_id=device, device_id_type=MESH
    )


def pieces(rows, cols):
    if cols == FF:
        wide = FF // 6
        return [[(slice(NIL, rows), slice((h * 3 + r) * wide, (h * 3 + r + 1) * wide)) for r in THIRDS] for h in PAIR]
    third, half = rows // 3, cols // 2
    return [[(slice(r * third, (r + 1) * third), slice(h * half, (h + 1) * half)) for r in THIRDS] for h in PAIR]


class Gather:
    copies = 19

    def __init__(self, here, own, full, parts, sems, base, turned=NIL, rest=False):
        self.rest = rest
        self.here, self.own, self.full, self.parts = here, own, full, parts
        self.sems, self.base = sems, base
        self.turns = [TURNS[(r + turned) % 3] for r in THIRDS]

    def view(self, how, r):
        return self.full.at[self.here.at([(b, how.get(b, "m")) for b in BITS]) + self.parts[r]]

    def hop(self, p, r):
        d = self.turns[r]
        dst = self.view({b: "f" for b in d[:p]}, r)
        src = self.own.at[self.parts[r]] if p == NIL else dst
        return send(src, dst, self.sems, self.base + p * 3 + r, self.here.peer(d[p]))

    def across(self, p, r):
        d = self.turns[r]
        ref = self.view({**{b: "f" for b in d[:p]}, d[p]: "o"}, r)
        return send(ref, ref, self.sems, self.base + 9 + p * 3 + r, self.here.peer(1))

    def place(self):
        return self.full.at[self.here.at([(b, "m") for b in BITS])]

    def own_across(self):
        return send(self.own, self.place(), self.sems, self.base + 18, self.here.peer(1))

    def keep(self):
        return pltpu.make_async_copy(self.own, self.place(), self.sems.at[2, self.base])

    def begin(self):
        for r in THIRDS:
            self.hop(NIL, r).start()
        if not self.rest:
            self.keep().start()
            self.own_across().start()

    def onward(self, p):
        if p == NIL and not self.rest:
            self.keep().wait()
        for r in THIRDS:
            self.hop(p, r).wait_recv()
            if p < 2:
                self.hop(p + 1, r).start()
            self.across(p, r).start()

    def arrived(self):
        for p in THIRDS:
            for r in THIRDS:
                self.across(p, r).wait_recv()
        if not self.rest:
            self.own_across().wait_recv()

    def finish(self):
        for p in THIRDS:
            for r in THIRDS:
                self.hop(p, r).wait_send()
                self.across(p, r).wait_send()
        if not self.rest:
            self.own_across().wait_send()


def cuts(widths, lead):
    out, at = [], NIL
    for w in widths:
        out.append((slice(None),) * lead + (slice(at, at + w),))
        at += w
    return out


class Scatter:
    peers = AXES
    n_out = 1

    def __init__(self, sums, number, lag=0.0, halves=(NIL, 1), ready=None, shape=None):
        self.array, self.number, self.halves = sums, number, halves
        self.rows, self.cols = shape or sums.shape[4:]
        self.lag, self.ready = lag, ready
        self.n_in = NIL if ready else 1

    def inputs(self):
        return [] if self.ready else [(self.array, ANY)]

    def outputs(self):
        spec = pl.BlockSpec((self.rows, self.width()), lambda *_: (NIL, NIL), pipeline_mode=pl.Buffered(1))
        return [(jax.ShapeDtypeStruct((self.rows, self.width()), BF16), spec)]

    def width(self):
        return self.cols * len(self.halves) // 2

    def scratch(self):
        r, c = pieces(self.rows, self.cols)[NIL][NIL]
        r, c = r.stop - r.start, c.stop - c.start
        legs = [pltpu.VMEM((3 * len(self.halves), *lead, r, c), BF16) for lead in ((2, 2), (2,), ())]
        return [pltpu.VMEM((2, 2, 2, self.rows, self.width()), F32), *legs, *legs, pltpu.SemaphoreType.DMA((2, 18)), pltpu.SemaphoreType.DMA]

    def events(self, here, ins, outs, scratch):
        (out,) = outs
        held, *legs, wire, local = scratch
        self.held = held
        going, coming = legs[:3], legs[3:]
        parts = pieces(self.rows, self.cols)
        if not self.ready:
            sums = ins[NIL]
        if len(self.halves) == 1:
            sums = sums.at[:, :, :, :, :, pl.ds(self.halves[NIL] * self.width(), self.width())]
        load = None if self.ready else pltpu.make_async_copy(sums.at[self.number], held, local)

        def place(order, picks):
            where = dict(zip(order, picks, strict=True))
            return tuple(where[b] for b in AXES)

        def hop(p, h, r):
            q = h * 3 + r
            return send(going[p].at[q], coming[p].at[q], wire, p * 6 + q, here.peer(TURNS[r][p]))

        count = len(self.halves)

        def begin():
            load.start()

        def first(h):
            if h == NIL and load:
                load.wait()
            for r in THIRDS:
                d, q = TURNS[r], h * 3 + r
                for i in PAIR:
                    for j in PAIR:
                        going[NIL][q, i, j] = held[place(d, (1 - here.bit[d[NIL]], i, j)) + parts[h][r]].astype(BF16)
                hop(NIL, h, r).start()

        def onward(p, h):
            for r in THIRDS:
                d, q = TURNS[r], h * 3 + r
                mine = [here.bit[b] for b in d]
                hop(p, h, r).wait_recv()
                if p == NIL:
                    for j in PAIR:
                        at = place(d, (mine[NIL], 1 - mine[1], j)) + parts[h][r]
                        going[1][q, j] = (held[at] + coming[NIL][q, 1 - mine[1], j].astype(F32)).astype(BF16)
                    hop(1, h, r).start()
                    for j in PAIR:
                        at = place(d, (mine[NIL], mine[1], j)) + parts[h][r]
                        held[at] = held[at] + coming[NIL][q, mine[1], j].astype(F32)
                elif p == 1:
                    at = place(d, (mine[NIL], mine[1], 1 - mine[2])) + parts[h][r]
                    going[2][q] = (held[at] + coming[1][q, 1 - mine[2]].astype(F32)).astype(BF16)
                    hop(2, h, r).start()
                    at = place(d, mine) + parts[h][r]
                    held[at] = held[at] + coming[1][q, mine[2]].astype(F32)
                else:
                    at = place(d, mine) + parts[h][r]
                    out[parts[h][r]] = (held[at] + coming[2][q].astype(F32)).astype(BF16)

        def finish():
            for p in THIRDS:
                for h in range(count):
                    for r in THIRDS:
                        hop(p, h, r).wait_send()

        times = {(NIL, NIL): 12.0, (NIL, 1): 19.0, (1, NIL): 23.0, (1, 1): 26.5, (2, NIL): 28.5, (2, 1): 30.0}
        if count == 1:
            times = {(NIL, NIL): 12.0, (1, NIL): 17.5, (2, NIL): 21.0}
        if self.ready:
            out_events = [(step, functools.partial(first, h)) for h, step in enumerate(self.ready)]
        else:
            out_events = [(self.lag, begin)] + [(self.lag + HOP_US + h / 2, functools.partial(first, h)) for h in range(count)]
        for (p, h), t in times.items():
            out_events.append((self.lag + t, functools.partial(onward, p, h)))
        out_events.append((1e9, finish))
        return out_events


class Total:
    peers = "all"
    n_out = 1

    def __init__(self, blocks):
        self.blocks = blocks
        self.n_in = len(blocks)

    def inputs(self):
        return [whole(b) for b in self.blocks]

    def outputs(self):
        return [(jax.ShapeDtypeStruct((8, 128), F32), pl.BlockSpec((8, 128), lambda *_: (NIL, NIL)))]

    def scratch(self):
        return [pltpu.VMEM((16, 8, 128), F32), pltpu.SemaphoreType.DMA((2, 16))]

    def run(self, here, ins, outs, scratch, lasts):
        (all_sums, sems), (out,) = scratch, outs

        def squares(ref):
            rows, cols = ref.shape

            def step(i, acc):
                g = ref[pl.ds(pl.multiple_of(i * 16, 16), 16), :].astype(F32)
                g = g * g
                return acc + sum(g[:, k * 128 : (k + 1) * 128] for k in range(cols // 128))

            s = lax.fori_loop(NIL, rows // 16, step, jnp.zeros((16, 128), F32))
            return s[:8] + s[8:]

        total = sum(squares(ref) for ref in (*ins, *lasts))
        all_sums[here.me] = total
        copies = []
        for k in range(1, 16):
            to = lax.rem(here.me + k, 16)
            copies.append(send(all_sums.at[here.me], all_sums.at[here.me], sems, k, {"dp": to}))
        for c in copies:
            c.start()
        for c in copies:
            c.wait()
        total = all_sums[NIL]
        for k in range(1, 16):
            total = total + all_sums[k]
        out[...] = jnp.full((8, 128), jnp.sum(total), F32)


def stage(cid, name, steps, step_us, body, ins, outs, scratch=(), own_peers=(), comms=(), total=None, flops=NIL):
    comms = list(comms)
    everyone = comms + ([total] if total else [])
    args = [*ins] + [x for c in everyone for x in c.inputs()]
    results = [*outs] + [x for c in everyone for x in c.outputs()]
    temps = [*scratch] + [x for c in everyone for x in c.scratch()]
    peers = sorted({b for c in comms for b in c.peers} | set(own_peers))

    def kernel(*refs):
        here = Here()
        i, o = refs[: len(args)], refs[len(args) : len(args) + len(results)]
        s = refs[len(args) + len(results) :]
        at = pl.program_id(NIL)

        def barrier():
            sem = pltpu.get_barrier_semaphore()
            if total:
                for k in range(1, 16):
                    pl.semaphore_signal(sem, inc=1, device_id={"dp": lax.rem(here.me + k, 16)}, device_id_type=MESH)
                pl.semaphore_wait(sem, 15)
            else:
                for b in peers:
                    pl.semaphore_signal(sem, inc=1, device_id=here.peer(b), device_id_type=MESH)
                pl.semaphore_wait(sem, len(peers))

        events, ni, no, ns = [], len(ins), len(outs), len(scratch)
        for c in comms:
            ci, co, cs = i[ni : ni + c.n_in], o[no : no + c.n_out], s[ns : ns + len(c.scratch())]
            ni, no, ns = ni + c.n_in, no + c.n_out, ns + len(c.scratch())
            events += c.events(here, ci, co, cs)
        events.sort(key=lambda e: e[NIL] * step_us if isinstance(e[NIL], int) else e[NIL])
        by_step = {}
        for t, fn in events:
            k = t if isinstance(t, int) else int(t / step_us + 0.8)
            by_step.setdefault(min(steps, k) if t < 1e9 else steps + 1, []).append(fn)

        def run(fns):
            for fn in fns:
                fn()

        @pl.when(at == NIL)
        def _():
            if peers or total:
                barrier()
            run(by_step.get(NIL, []))

        for k in range(1, steps):
            if k in by_step:
                pl.when(at == k)(functools.partial(run, by_step[k]))
        if body:
            body(here, at, i[: len(ins)], o[: len(outs)], s[: len(scratch)])

        @pl.when(at == steps - 1)
        def _():
            run(by_step.get(steps, []) + by_step.get(steps + 1, []))
            if total:
                total.run(here, i[ni:], o[no:], s[ns:], o[len(outs) : no])

    got = pl.pallas_call(
        kernel,
        grid=(steps,),
        in_specs=[spec for _, spec in args],
        out_specs=[spec for _, spec in results],
        out_shape=[shape for shape, _ in results],
        scratch_shapes=temps,
        compiler_params=pltpu.CompilerParams(
            collective_id=cid if (peers or total) else None, has_side_effects=bool(peers or total), vmem_limit_bytes=63 * 1024 * 1024
        ),
        name=name,
    )(*[a for a, _ in args])
    return got


def whole(array):
    return (array, pl.BlockSpec(array.shape, lambda *_: (NIL,) * array.ndim, pipeline_mode=pl.Buffered(1)))


def by_rows(array, height):
    return (array, pl.BlockSpec((height, array.shape[1]), lambda i: (i, NIL)))


def new(shape, dtype, block, index):
    return (jax.ShapeDtypeStruct(shape, dtype), pl.BlockSpec(block, index))


def mm(a, b):
    return lax.dot_general(a, b, (((1,), (NIL,)), ((), ())), preferred_element_type=F32)


def mm_nt(a, b):
    return lax.dot_general(a, b, (((1,), (1,)), ((), ())), preferred_element_type=F32)


def norm_of(wide):
    scale = lax.rsqrt(jnp.mean(wide * wide, -1, keepdims=True) + 1e-6)
    return (wide * scale).astype(BF16)


COL = lambda s: (NIL, s)
ROW = lambda i: (i, NIL)


def sigmoid(g):
    return 0.5 * jnp.tanh(0.5 * g) + 0.5


def by_core(blocks, out, cols):
    rows = out.shape[2]
    for k in range(out.shape[1]):
        for c in PAIR:
            at = (2 * k + c) * rows
            out[c, k, :, cols] = blocks[at : at + rows, :]


WIDE = SPAN
UNITS = FF // WIDE
KINDS = 2, D // 16
CHUNK = FF // 3
WIRE_GU, WIRE_D = 16.8, 8.4
HOP_US, EARLY_US = 2.5, 6.0
CUT_GU, CUT_D = (384, 384, SPAN), (512, 384, 384)
PLACES = (2, 2, 2, 2)


def all_rows(fn):
    count = TOKENS // SPAN // 2

    def turn(j, _):
        for i in range(count):
            fn(pl.ds(pl.multiple_of((j * count + i) * SPAN, SPAN), SPAN))
        return NIL

    lax.fori_loop(NIL, 2, turn, NIL)


def tile_of(gu, c, which, q):
    return gu[c, :, :, :, :, which, :, pl.ds(pl.multiple_of(q * WIDE, WIDE), WIDE)].reshape(D, WIDE)


def by_third(block, out, c):
    out[...] = jnp.concatenate([block[:, n * 192 + c * 64 : n * 192 + c * 64 + 64] for n in range(16)], axis=1)


def barrier_of(here, peers):
    sem = pltpu.get_barrier_semaphore()
    for b in peers:
        pl.semaphore_signal(sem, inc=1, device_id=here.peer(b), device_id_type=MESH)
    pl.semaphore_wait(sem, len(peers))


def schedule(at, steps, table):
    by_step = {}
    for k, fn in table:
        by_step.setdefault(k, []).append(fn)
    for k, fns in by_step.items():

        @pl.when(at == k)
        def _(fns=fns):
            for fn in fns:
                fn()


def wire_order(units):
    legs = [("b", NIL)]
    for n in range(len(units)):
        legs += [("b", n + 1), (NIL, n + 1) if n else (NIL, NIL)] if n else [("b", 1), (NIL, NIL), ("b", 2), (NIL, 1)]
        legs += [(1, n)]
    order, seen = [], set()
    for leg in legs + [(NIL, n) for n in range(len(units))]:
        if leg not in seen and leg[1] < len(units):
            seen.add(leg)
            order.append(leg)
    wire, done, out, last = 0.0, {}, [], 0.0
    for kind, n in order:
        length, unit = units[n]
        if kind == "b":
            out.append((last, unit.begin, unit))
            wire = max(wire, last) + length / 7
            done[NIL, n] = wire
        else:
            last = max(last, done[kind, n] + HOP_US)
            out.append((last, functools.partial(unit.onward, kind), unit))
            wire = max(wire, last) + length * (2, 4)[kind] / 7
            done[kind + 1, n] = wire
    for n, (_, unit) in enumerate(units):
        unit.ready = done[2, n] + 4.0
        out.append((done[2, n] + HOP_US, functools.partial(unit.onward, 2), unit))
    return sorted(out, key=lambda e: e[NIL])


def placed(events, lengths, due):
    starts, now = [], 0.0
    for i, length in enumerate(lengths):
        now = max([now] + [unit.ready for step, unit in due if step == i])
        starts.append(now)
        now += length
    out = []
    for t, fn, unit in events:
        k = next((i for i, u in enumerate(starts) if u >= t - EARLY_US), len(starts))
        out.append((min([k] + [step for step, one in due if one is unit]), fn))
    return out


def call(cid, name, kernel, steps, ins, outs, scratch):
    return pl.pallas_call(
        kernel,
        grid=(steps,),
        in_specs=[spec for _, spec in ins],
        out_specs=[spec for _, spec in outs],
        out_shape=[shape for shape, _ in outs],
        scratch_shapes=scratch,
        compiler_params=pltpu.CompilerParams(collective_id=cid, has_side_effects=True, vmem_limit_bytes=67043328),
        name=name,
    )(*[a for a, _ in ins])


def blocks_of(array, *index):
    lead = len(index)
    block = (1,) * lead + array.shape[lead:]
    rest = (NIL,) * (array.ndim - lead)
    return (array, pl.BlockSpec(block, lambda s: index + rest, pipeline_mode=pl.Buffered(1)))


N1 = 8
G1 = N1 + UNITS
D1 = G1 + 4
E1 = D1 + 8


def first_stage(cid, x, wg, wu, wd):
    def kernel(x, wg, wu, wg1, wu1, wd_own, wd1_own, a_t, g_out, u_out, act_t, wd_full, h_out, a1_out, a1_t, gu1_full, wd1_full, *scratch):
        a, gu_all, wd_all, act, gu_own, gu1_own, sems, local = scratch
        wd_own, wd1_own = wd_own.at[NIL], wd1_own.at[NIL]
        here, at = Here(), pl.program_id(NIL)

        @pl.when(at == NIL)
        def _():
            for k, own in enumerate((wg, wu)):
                block = own[NIL]
                for c in THIRDS:
                    by_third(block, gu_own.at[c, k], c)
            for k, own in enumerate((wg1, wu1)):
                by_third(own[NIL], gu1_own.at[k], NIL)

        n = Gather.copies
        units = [Gather(here, gu_own.at[c], gu_all.at[c], cuts(CUT_GU, 2), sems, c * n, c) for c in THIRDS]
        halves = pieces(D3, D)
        units += [Gather(here, wd_own, wd_all, halves[h], sems, (3 + h) * n, rest=h == 1) for h in PAIR]
        units += [Gather(here, gu1_own, gu1_full, cuts(CUT_GU, 2), sems, 5 * n)]
        units += [Gather(here, wd1_own, wd1_full, cuts(CUT_D, 1), sems, 6 * n, 2)]

        timed = [(WIRE_D if i == 6 else WIRE_D * 1.5 if i in (3, 4) else WIRE_GU, unit) for i, unit in enumerate(units)]
        lengths = [1.0] * N1 + [3.6] * UNITS + [5.0] * (D1 - G1) + [1.0] * N1
        due = [(N1, units[NIL]), (N1 + 4, units[1]), (N1 + 8, units[2]), (G1, units[3]), (G1 + 2, units[4])]
        events = placed(wire_order(timed), lengths, due)
        waits = [(k, unit.arrived) for k, unit in due]
        spill = pltpu.make_async_copy(wd_all, wd_full, local)

        schedule(at, E1, [(NIL, functools.partial(barrier_of, here, BITS))])
        schedule(at, E1, [e for e in events if e[NIL] < E1])
        schedule(at, E1, waits)

        @pl.when(at < N1)
        def _():
            normed = norm_of(x[...].astype(F32))
            a[pl.ds(pl.multiple_of(at * SPAN, SPAN), SPAN), :] = normed
            by_core(normed.T, a_t, slice(None))

        @pl.when((at >= N1) & (at < G1))
        def _():
            t = at - N1
            c, q = lax.div(t, 4), lax.rem(t, 4)
            def part(rows):
                g = mm(a[rows, :], tile_of(gu_all, c, NIL, q))
                u = mm(a[rows, :], tile_of(gu_all, c, 1, q))
                v = (g * sigmoid(g) * u).astype(BF16)
                g_out[rows, :] = g
                u_out[rows, :] = u
                act[t, rows, :] = v
                by_core(v.T, act_t, rows)

            all_rows(part)

        @pl.when((at >= G1) & (at < D1))
        def _():
            t = at - G1
            cols = pl.ds(pl.multiple_of(lax.div(t, 2) * 640, 128), 640)
            for i in range(4):
                rows = pl.ds(pl.multiple_of(lax.rem(t, 2) * 1024 + i * SPAN, SPAN), SPAN)
                y = jnp.zeros((SPAN, 640), F32)
                for c in THIRDS:
                    left = jnp.concatenate([act[c * 4 + q, rows, :] for q in range(4)], axis=1)
                    y = y + mm(left, wd_all[:, :, :, :, c * 64 : (c + 1) * 64, cols].reshape(CHUNK, 640))
                a[rows, cols] = y.astype(BF16)

        @pl.when(at == D1)
        def _():
            spill.start()

        @pl.when(at >= D1)
        def _():
            h = x[...] + a[pl.ds(pl.multiple_of((at - D1) * SPAN, SPAN), SPAN), :]
            h_out[...] = h
            normed = norm_of(h.astype(F32))
            a1_out[...] = normed
            by_core(normed.T, a1_t, slice(None))

        @pl.when(at == E1 - 1)
        def _():
            for k, fn in events:
                if k >= E1:
                    fn()
            for unit in units[5:]:
                unit.arrived()
            for unit in units:
                unit.finish()
            spill.wait()

    D3 = FF // 16
    tile = lambda s: jnp.clip(s - N1, NIL, UNITS - 1)
    early = lambda s: jnp.minimum(s, N1 - 1)
    late = lambda s: jnp.maximum(s - D1, NIL)
    strip = (2, 8, D // 16, TOKENS)
    outs = [
        new(strip, BF16, (*strip[:3], SPAN), lambda s: (NIL, NIL, NIL, early(s))),
        new((TOKENS, FF), F32, (TOKENS, WIDE), lambda s: (NIL, tile(s))),
        new((TOKENS, FF), F32, (TOKENS, WIDE), lambda s: (NIL, tile(s))),
        new((2, 8, D3, TOKENS), BF16, (2, 2, 64, TOKENS), lambda s: (NIL, lax.rem(tile(s), 4), lax.div(tile(s), 4), NIL)),
        (jax.ShapeDtypeStruct((*PLACES, D3, D), BF16), ANY),
        new((TOKENS, D), BF16, (SPAN, D), lambda s: (late(s), NIL)),
        new((TOKENS, D), BF16, (SPAN, D), lambda s: (late(s), NIL)),
        new(strip, BF16, (*strip[:3], SPAN), lambda s: (NIL, NIL, NIL, late(s))),
        (jax.ShapeDtypeStruct((*PLACES, *KINDS, CHUNK), BF16), ANY),
        (jax.ShapeDtypeStruct((*PLACES, 64, D), BF16), ANY),
    ]
    ins = [(x, pl.BlockSpec((SPAN, D), lambda s: (jnp.where(s < D1, early(s), late(s)), NIL)))]
    ins += [blocks_of(wg, NIL), blocks_of(wu, NIL), blocks_of(wg, 1), blocks_of(wu, 1), blocks_of(wd, NIL)]
    ins += [(wd, pl.BlockSpec((1, 64, D), lambda s: (1, NIL, NIL), pipeline_mode=pl.Buffered(1)))]
    scratch = [
        pltpu.VMEM((TOKENS, D), BF16),
        pltpu.VMEM((3, *PLACES, *KINDS, CHUNK), BF16),
        pltpu.VMEM((*PLACES, D3, D), BF16),
        pltpu.VMEM((UNITS, TOKENS, WIDE), BF16),
        pltpu.VMEM((3, *KINDS, CHUNK), BF16),
        pltpu.VMEM((*KINDS, CHUNK), BF16),
        pltpu.SemaphoreType.DMA((3, 7 * Gather.copies)),
        pltpu.SemaphoreType.DMA,
    ]
    return call(cid, "first", kernel, E1, ins, outs, scratch)


def second_stage(cid, a, dy, wg, wu, wd, gu_first, wd_first):
    def kernel(a_in, dy_in, wg, wu, wd_own, gu_first, wd_first, dgu, act_t, gu_rest, *scratch):
        gu_all, wd_all, gu_own, a, dy, sems, local = scratch
        wd_own = wd_own.at[NIL]
        here, at = Here(), pl.program_id(NIL)

        @pl.when(at == NIL)
        def _():
            for k, own in enumerate((wg, wu)):
                block = own[NIL]
                for c in (1, 2):
                    by_third(block, gu_own.at[c - 1, k], c)

        n = Gather.copies
        units = []
        for c in (1, 2):
            units.append(Gather(here, gu_own.at[c - 1], gu_all.at[c], cuts(CUT_GU, 2), sems, len(units) * n, c))
            units.append(Gather(here, wd_own.at[pl.ds(c * 64, 64)], wd_all.at[c], cuts(CUT_D, 1), sems, len(units) * n, c + 2))
        timed = list(zip((WIRE_GU, WIRE_D) * 2, units, strict=True))
        due = [(4, units[NIL]), (4, units[1]), (8, units[2]), (8, units[3])]
        events = placed(wire_order(timed), [5.6] * UNITS, due)
        moves = ((a_in, a), (gu_first, gu_all.at[NIL]), (dy_in, dy), (wd_first, wd_all.at[NIL]))
        loads = [pltpu.make_async_copy(src, dst, local.at[i]) for i, (src, dst) in enumerate(moves)]
        spills = [pltpu.make_async_copy(gu_all.at[c], gu_rest.at[c - 1], local.at[3 + c]) for c in (1, 2)]
        table = [(NIL, load.start) for load in loads] + [(NIL, functools.partial(barrier_of, here, BITS))]
        table += [e for e in events if e[NIL] < UNITS]
        table += [(NIL, load.wait) for load in loads]
        table += [(k, unit.arrived) for k, unit in due] + [(4, spills[NIL].start), (8, spills[1].start)]
        schedule(at, UNITS, table)

        c, q = lax.div(at, 4), lax.rem(at, 4)
        qx, qy = lax.div(q, 2), lax.rem(q, 2)
        def part(rows):
            g = mm(a[rows, :], tile_of(gu_all, c, NIL, q))
            u = mm(a[rows, :], tile_of(gu_all, c, 1, q))
            dact = mm_nt(dy[rows, :], wd_all[c, qx, qy].reshape(WIDE, D)).astype(BF16).astype(F32)
            s = sigmoid(g)
            silu = g * s
            by_core((silu * u).astype(BF16).T, act_t, rows)
            dgu[NIL, rows, :] = (dact * u * (s + silu * (1.0 - s))).astype(BF16)
            dgu[1, rows, :] = (dact * silu).astype(BF16)

        all_rows(part)

        @pl.when(at == UNITS - 1)
        def _():
            for unit in units:
                unit.finish()
            for s in spills:
                s.wait()

    outs = [
        new((2, TOKENS, FF), BF16, (2, TOKENS, WIDE), lambda s: (NIL, NIL, s)),
        new((2, 8, FF // 16, TOKENS), BF16, (2, 2, 64, TOKENS), lambda s: (NIL, lax.rem(s, 4), lax.div(s, 4), NIL)),
        (jax.ShapeDtypeStruct((2, *PLACES, *KINDS, CHUNK), BF16), ANY),
    ]
    ins = [(a, ANY), (dy, ANY), blocks_of(wg, 1), blocks_of(wu, 1), blocks_of(wd, 1), (gu_first, ANY), (wd_first, ANY)]
    scratch = [
        pltpu.VMEM((3, *PLACES, *KINDS, CHUNK), BF16),
        pltpu.VMEM((3, *PLACES, 64, D), BF16),
        pltpu.VMEM((2, *KINDS, CHUNK), BF16),
        *[pltpu.VMEM((TOKENS, D), BF16)] * 2,
        pltpu.SemaphoreType.DMA((3, 4 * Gather.copies)),
        pltpu.SemaphoreType.DMA((6,)),
    ]
    return call(cid, "second", kernel, UNITS, ins, outs, scratch)


def dact_stage(cid, dy, wd, g, u, comms):
    def body(here, at, ins, outs, scratch):
        dy, wd, g_in, u_in = ins
        def part(rows):
            dact = mm_nt(dy[rows, :], wd[...].reshape(WIDE, D)).astype(BF16).astype(F32)
            g, u = g_in[rows, :], u_in[rows, :]
            s = sigmoid(g)
            silu = g * s
            outs[NIL][NIL, rows, :] = (dact * u * (s + silu * (1.0 - s))).astype(BF16)
            outs[NIL][1, rows, :] = (dact * silu).astype(BF16)

        all_rows(part)

    outs = [new((2, TOKENS, FF), BF16, (2, TOKENS, WIDE), lambda s: (NIL, NIL, s))]
    tile = pl.BlockSpec((TOKENS, WIDE), COL)
    ins = [whole(dy), (wd, pl.BlockSpec((4, 64, D), lambda s: (lax.rem(s, 4), lax.div(s, 4), NIL))), (g, tile), (u, tile)]
    return stage(cid, "dact", UNITS, 2.5, body, ins, outs, comms=comms)


def dinput_stage(cid, dgu, gu_first, gu_rest, h, dy, comms):
    def body(here, at, ins, outs, scratch):
        dgu, gu_first, gu_rest, h, dy = ins
        back = []
        for k in PAIR:
            total = mm_nt(dgu[k, :, :CHUNK], gu_first[:, :, :, :, k].reshape(D, CHUNK))
            for c in range(1, 3):
                total += mm_nt(dgu[k, :, c * CHUNK : (c + 1) * CHUNK], gu_rest[c - 1, :, :, :, :, k].reshape(D, CHUNK))
            back.append(total.astype(BF16))
        da = (back[NIL] + back[1]).astype(F32)
        wide = h[...].astype(F32)
        scale = lax.rsqrt(jnp.mean(wide * wide, -1, keepdims=True) + 1e-6)
        along = jnp.mean(da * wide, -1, keepdims=True)
        dh = da * scale - wide * (scale * scale * scale * along)
        outs[NIL][...] = dy[...] + dh.astype(BF16)

    outs = [new((TOKENS, D), BF16, (SPAN, D), ROW)]
    ins = [(dgu, pl.BlockSpec((2, SPAN, FF), lambda i: (NIL, i, NIL))), whole(gu_first), whole(gu_rest), by_rows(h, SPAN), by_rows(dy, SPAN)]
    return stage(cid, "dinput", 8, 5.2, body, ins, outs, comms=comms)


def dw_stage(cid, left, right, comms, into=(), total=None):
    rows, (count, _, n) = left.shape[2], right.shape
    width = 512 if n == FF else SPAN
    per = n // width
    turn = 2 * per

    def body(here, at, ins, outs, scratch):
        left_in, right = ins
        left, going, coming, sems, local = scratch
        core = here.bit[1]
        step = 4 if rows == 80 else 2
        matrix, place = lax.div(at, turn), lax.rem(at, turn)

        def load(c):
            return pltpu.make_async_copy(left_in.at[c], left.at[c], local.at[c])

        @pl.when(at == NIL)
        def _():
            load(1 - core).start()
            load(core).start()
            load(1 - core).wait()

        @pl.when(at == per)
        def _():
            load(core).wait()

        def swap(t):
            one = matrix * per + t
            return send(going.at[t], coming.at[one], sems, one, here.peer(1))

        @pl.when(place < per)
        def _():
            for k in range(NIL, 8, step):
                a = left[1 - core, k : k + step].reshape(step * rows, TOKENS)
                going[place, k : k + step] = mm(a, right[NIL]).astype(BF16).reshape(step, rows, width)
            swap(place).start()

        def own(put):
            t = place - per
            swap(t).wait()
            for k in range(NIL, 8, step):
                a = left[core, k : k + step].reshape(step * rows, TOKENS)
                got = mm(a, right[NIL]).reshape(step, rows, width)
                for i in range(step):
                    where = (k + i) // 4, (k + i) // 2 % 2, (k + i) % 2
                    put(where, t, got[i] + coming[matrix * per + t, k + i].astype(F32))

        def put_out(where, t, value):
            outs[NIL][(NIL, *where)] = value

        if into:
            for m, scatter in enumerate(into):

                def put_held(where, t, value, held=scatter.held):
                    held[(*where, slice(None), pl.ds(pl.multiple_of(t * width, width), width))] = value

                pl.when((place >= per) & (matrix == m))(functools.partial(own, put_held))
        else:
            pl.when(place >= per)(functools.partial(own, put_out))

    def source(s):
        return (lax.div(s, turn), NIL, lax.rem(lax.rem(s, turn), per))

    def back(s):
        return (lax.div(s, turn), NIL, NIL, NIL, NIL, jnp.maximum(lax.rem(s, turn) - per, NIL))

    outs = [] if into else [new((count, 2, 2, 2, rows, n), F32, (1, 2, 2, 2, rows, width), back)]
    scratch = [pltpu.VMEM(left.shape, BF16), pltpu.VMEM((per, 8, rows, width), BF16), pltpu.VMEM((count * per, 8, rows, width), BF16)]
    scratch += [pltpu.SemaphoreType.DMA((2, count * per)), pltpu.SemaphoreType.DMA((2,))]
    ins = [(left, ANY), (right, pl.BlockSpec((1, TOKENS, width), source))]
    steps = count * turn
    return stage(cid, "dw", steps, count * 21.0 / steps, body, ins, outs, scratch, own_peers=(1,), comms=[*comms, *into], total=total)


def update_stage(weights, moments, seconds, sums, squares):
    steps = 5
    flat = [piece for pair in sums for layer in pair for piece in layer]
    count = 16 * sum(w.size for w in weights)

    def kernel(*refs):
        squares, ws, ms, vs = refs[NIL], refs[1:4], refs[4:7], refs[7:10]
        pieces_in, outs = list(refs[10 : 10 + len(flat)]), refs[10 + len(flat) :]
        factor = jnp.minimum(1.0, 0.5 * lax.rsqrt(squares[...] / count + 1e-30))[:1, :1]
        for i in THIRDS:
            for n in PAIR:
                taken = [pieces_in.pop(NIL) for _ in sums[i][n]]
                g = jnp.concatenate([r[...].astype(F32) for r in taken], axis=1) if len(taken) > 1 else taken[NIL][...].astype(F32)
                if i < 2:
                    at = [c * CHUNK + k * 64 for k in range(16) for c in THIRDS]
                    g = jnp.concatenate([g[:, u : u + 64] for u in at], axis=1)
                g = g * factor
                m = 0.9 * ms[i][n] + 0.1 * g
                v = 0.95 * vs[i][n] + 0.05 * g * g
                w = ws[i][n].astype(F32)
                outs[i][n] = (w - 0.02 * (m * lax.rsqrt(v + 1e-8) + 0.1 * w)).astype(BF16)
                outs[3 + i][n] = m
                outs[6 + i][n] = v

    def spec(array):
        lead = array.ndim - 2
        rows, cols = array.shape[lead:]
        height = 16 if rows == D // 16 else 48
        last = rows // height - 1
        return pl.BlockSpec((2,) * lead + (height, cols), lambda s: (NIL,) * lead + (jnp.minimum(s, last), NIL))

    args = [*weights, *moments, *seconds, *flat]
    like = [*weights, *moments, *seconds]
    return pl.pallas_call(
        kernel,
        grid=(steps,),
        in_specs=[pl.BlockSpec((8, 128), lambda s: (NIL, NIL))] + [spec(a) for a in args],
        out_specs=[spec(a) for a in like],
        out_shape=[jax.ShapeDtypeStruct(a.shape, a.dtype) for a in like],
        compiler_params=pltpu.CompilerParams(vmem_limit_bytes=60 * 1024 * 1024),
        name="update",
    )(squares, *args)


def solution(mesh):
    def step(x, dy, *arrays):
        weights, m, v = (arrays[i : i + 3] for i in (NIL, 3, 6))
        wg, wu, wd = weights
        x, dy = x[NIL], dy[NIL]
        a0_t, g0, u0, act0_t, wd0, h1, a1, a1_t, gu1_first, wd1_first = first_stage(NIL, x, wg, wu, wd)
        dgu1, act1_t, gu1_rest = second_stage(1, a1, dy, wg, wu, wd, gu1_first, wd1_first)
        (s_d1,) = dw_stage(9, act1_t, dy[None], [])
        s_1, r_d1 = dw_stage(2, a1_t, dgu1, [Scatter(s_d1, NIL)])
        dh1, r_g1 = dinput_stage(3, dgu1, gu1_first, gu1_rest, h1, dy, [Scatter(s_1, NIL)])
        s_d0, r_u1a = dw_stage(4, act0_t, dh1[None], [Scatter(s_1, 1, halves=(NIL,))])
        early = [Scatter(s_1, 1, halves=(1,)), Scatter(s_d0, NIL, 11.0, halves=(NIL,))]
        dgu0, r_u1b, r_d0a = dact_stage(5, dh1, wd0.reshape(16, FF // 16, D), g0, u0, early)
        block = (D // 16, FF)
        late = [Scatter(None, NIL, 14.0, ready=(9, 12), shape=block), Scatter(None, NIL, 40.0, ready=(21, 24), shape=block)]
        total = Total([r_d1, r_g1, r_u1a, r_u1b, r_d0a])
        r_d0b, r_g0, r_u0, squares = dw_stage(6, a0_t, dgu0, [Scatter(s_d0, NIL, halves=(1,))], late, total)
        sums = (((r_g0,), (r_g1,)), ((r_u0,), (r_u1a, r_u1b)), ((r_d0a, r_d0b), (r_d1,)))
        return tuple(update_stage(weights, m, v, sums, squares))

    states, cut = P(("rep", "dp"), None, None), P(None, "dp", None)
    return jax.shard_map(
        step,
        mesh=mesh,
        in_specs=(states, states) + (cut,) * 9,
        out_specs=(P("rep", "dp", None),) * 9,
        check_vma=False,
    )
```

time: 955 us -> 540 us (0.57)
  Pallas kernels: 0 us -> 531 us
  waiting for transfers between devices: 445 us -> 0 us
  matrix products: 396 us -> 0 us
  other arithmetic: 33.3 us -> 0 us
  blocking collectives: 31.8 us -> 0 us
  local copies, waits for them, and re-layouts: 25.1 us -> 0 us
  between operations: 17.5 us -> 1.16 us
    pallas_call x0 -> x9, Pallas kernels: none -> 531 us  [the longest x6 289 us: stage(): pl.pallas_call(kernel, grid=(steps,), in_specs=[spec for _, spec in args]...]
    dot_general x15 -> x0, matrix products: 396 us -> none  [the longest x5 140 us: layer(): gate = jnp.dot(a, w['w_gate'], preferred_element_type=jnp.float32)]
    reduce_scatter x6 -> x0, waiting for transfers between devices: 298 us -> none  [step(): lax.psum_scatter(by_w[name], 'dp', scatter_dimension=0, tiled=True)]
    all_gather x6 -> x0, waiting for transfers between devices: 145 us -> none  [fetched(): lax.all_gather(w[number], 'dp', axis=0, tiled=True)]
    psum x1 -> x0, blocking collectives: 31.8 us -> none  [step(): squares = lax.psum(sum((jnp.sum(g * g) for g in gradients)), 'dp')]
    unnamed x38 -> x0, local copies, waits for them, and re-layouts: 18.5 us -> none
    add_any x1 -> x0, other arithmetic: 12.3 us -> none  [normed(): wide = h.astype(jnp.float32)]
    reduce_sum x4 -> x0, other arithmetic: 10.6 us -> none  [the longest x3 7.02 us: step(): squares = lax.psum(sum((jnp.sum(g * g) for g in gradients)), 'dp')]
  transfers between devices with their start and end apart: 12 -> 0, of which waited for: 10 -> 0; matrix products, arithmetic and copies ran while one was open for 33% -> 0% of each run, Pallas kernels for 0% -> 0%
where the time goes in v2:
time: 540 us; the launch traced here: 532 us
  Pallas kernels  531 us (98%)
    pallas_call x6, Pallas kernels, stage(): pl.pallas_call(kernel, grid=(steps,), in_specs=[spec for _, spec in args]...  289 us
    pallas_call x2, Pallas kernels, call(): pl.pallas_call(kernel, grid=(steps,), in_specs=[spec for _, spec in ins],...  227 us
    pallas_call x1, Pallas kernels, update_stage(): pl.pallas_call(kernel, grid=(steps,), in_specs=[pl.BlockSpec((8, 128), la...  15.5 us

profile of v2, /device:TPU:0, one launch (start us, length us, event | category | flops | bytes accessed | tf_op | source)
XLA Modules:
  0.0 532.3 jit_solution(1374081476656165867)
XLA Ops:
  0.6 134.6 %first.1 = (bf16[2,8,80,2048]{3,2,1,0:T(8,128)(2,1)}, f32[2048,3072]{1,0:T(8,128)}, f32[2048,3072]{1,0:T(8,128)}, bf16[2,8,192,2048]{3,2,1,0:T(8,128)(2,1)}, bf1...) custom-call(bf16[2048,1280]{1,0:T(8,128)(2,1)} %bitcast.8, ...), custom_call_target="tpu_custom_call" | custom-call | tf_op jit(solution)/shard_map/first/pallas_call | solution.py:477
  135.3 92.0 %second.1 = (bf16[2,2048,3072]{2,1,0:T(8,128)(2,1)}, bf16[2,8,192,2048]{3,2,1,0:T(8,128)(2,1)}, bf16[2,2,2,2,2,2,80,1024]{7,6,5,4,3,2,1,0:T(8,128)(2,1)}) custom-call(bf16[2048,1280]{1,0:T(8,128)(2,1)} %get-tuple-element.36.a_in, bf16[2048,1280]{1,0:T(8,128)(2,1)} %bitcast.4, bf16[2,80,3072]{2,1,0:T(8,128)(2,1)} %refs_1_.3, bf16[2,80,3072]{2,1,0:T(8,128)(2,1)} %refs_2_.1, ...), custom_call_target="tpu_custom_call" | custom-call | tf_op jit(solution)/shard_map/second/pallas_call | solution.py:477
  227.2 24.0 %dw.4.refs_2_ = f32[1,2,2,2,192,1280]{5,4,3,2,1,0:T(8,128)} custom-call(bf16[2,8,192,2048]{3,2,1,0:T(8,128)(2,1)} %get-tuple-element.43.refs_0_, bf16[1,2048,1280]{2,1,0:T(8,128)(2,1)} %refs_1_.2), custom_call_target="tpu_custom_call" | custom-call | tf_op jit(solution)/shard_map/dw/pallas_call | solution.py:331
  251.2 51.9 %dw.5 = (f32[2,2,2,2,80,3072]{5,4,3,2,1,0:T(8,128)}, bf16[192,1280]{1,0:T(8,128)(2,1)}) custom-call(bf16[2,8,80,2048]{3,2,1,0:T(8,128)(2,1)} %get-tuple-element.42.refs_0_, bf16[2,2048,3072]{2,1,0:T(8,128)(2,1)} %get-tuple-element.39.refs_1_.refs_0_, f32[1,2,2,2,192,1280]{5,4,3,2,1,0:T(8,128)} %dw.4.refs_2_), custom_call_target="tpu_custom_call" | custom-call | tf_op jit(solution)/shard_map/dw/pallas_call | solution.py:331
  303.1 51.5 %dinput.1 = (bf16[2048,1280]{1,0:T(8,128)(2,1)}, bf16[80,3072]{1,0:T(8,128)(2,1)}) custom-call(bf16[2,2048,3072]{2,1,0:T(8,128)(2,1)} %get-tuple-element.39.refs_1_.refs_0_, bf16[2,2,2,2,2,80,1024]{6,5,4,3,2,1,0:T(8,128)(2,1)} %get-tuple-element.37.gu_first.refs_1_, bf16[2,2,2,2,2,2,80,1024]{7,6,5,4,3,2,1,0:T(8,128)(2,1)} %get-tuple-element.40.refs_2_, ...), custom_call_target="tpu_custom_call" | custom-call | tf_op jit(solution)/shard_map/dinput/pallas_call | solution.py:331
  354.6 28.9 %dw.6 = (f32[1,2,2,2,192,1280]{5,4,3,2,1,0:T(8,128)}, bf16[80,1536]{1,0:T(8,128)(2,1)}) custom-call(bf16[2,8,192,2048]{3,2,1,0:T(8,128)(2,1)} %get-tuple-element.49.refs_0_, bf16[1,2048,1280]{2,1,0:T(8,128)(2,1)} %bitcast.6, f32[2,2,2,2,80,3072]{5,4,3,2,1,0:T(8,128)} %get-tuple-element.44.refs_5_.refs_2_.refs_4_), custom_call_target="tpu_custom_call" | custom-call | tf_op jit(solution)/shard_map/dw/pallas_call | solution.py:331
  383.5 45.7 %dact.1 = (bf16[2,2048,3072]{2,1,0:T(8,128)(2,1)}, bf16[80,1536]{1,0:T(8,128)(2,1)}, bf16[192,640]{1,0:T(8,128)(2,1)}) custom-call(bf16[2048,1280]{1,0:T(8,128)(2,1)} %get-tuple-element.45.refs_0_, bf16[16,192,1280]{2,1,0:T(8,128)(2,1)} %bitcast.7, f32[2048,3072]{1,0:T(8,128)} %get-tuple-element.47.refs_2_, f32[2048,3072]{1,0:T(8,128)} %get-tuple-element.48.refs_3_, ...), custom_call_target="tpu_custom_call" | custom-call | tf_op jit(solution)/shard_map/dact/pallas_call | solution.py:331
  429.2 87.1 %dw.7 = (bf16[192,640]{1,0:T(8,128)(2,1)}, bf16[80,3072]{1,0:T(8,128)(2,1)}, bf16[80,3072]{1,0:T(8,128)(2,1)}, f32[8,128]{1,0:T(8,128)}) custom-call(bf16[2,8,80,2048]{3,2,1,0:T(8,128)(2,1)} %get-tuple-element.35.refs_0_, bf16[2,2048,3072]{2,1,0:T(8,128)(2,1)} %get-tuple-element.51.refs_1_, f32[1,2,2,2,192,1280]{5,4,3,2,1,0:T(8,128)} %get-tuple-element.50.refs_5_.refs_2_, ...), custom_call_target="tpu_custom_call" | custom-call | tf_op jit(solution)/shard_map/dw/pallas_call | solution.py:331
  516.4 15.5 %update.1 = (bf16[2,80,3072]{2,1,0:T(8,128)(2,1)}, bf16[2,80,3072]{2,1,0:T(8,128)(2,1)}, bf16[2,192,1280]{2,1,0:T(8,128)(2,1)}, f32[2,80,3072]{2,1,0:T(8,128)}, ...) custom-call(f32[8,128]{1,0:T(8,128)} %get-tuple-element.57.refs_0_, ...), custom_call_target="tpu_custom_call" | custom-call | tf_op jit(solution)/shard_map/update/pallas_call | solution.py:839

commit v3 on v2

--- a/solution.py
+++ b/solution.py
@@ -389,7 +389,7 @@
 KINDS = 2, D // 16
 CHUNK = FF // 3
 WIRE_GU, WIRE_D = 16.8, 8.4
-HOP_US, EARLY_US = 2.5, 6.0
+HOP_US, EARLY_US = 2.5, 4.0
 CUT_GU, CUT_D = (384, 384, SPAN), (512, 384, 384)
 PLACES = (2, 2, 2, 2)
 
@@ -460,7 +460,7 @@
     return sorted(out, key=lambda e: e[NIL])
 
 
-def placed(events, lengths, due):
+def placed(events, lengths, due, early=EARLY_US):
     starts, now = [], 0.0
     for i, length in enumerate(lengths):
         now = max([now] + [unit.ready for step, unit in due if step == i])
@@ -468,7 +468,7 @@
         now += length
     out = []
     for t, fn, unit in events:
-        k = next((i for i, u in enumerate(starts) if u >= t - EARLY_US), len(starts))
+        k = next((i for i, u in enumerate(starts) if u >= t - early), len(starts))
         out.append((min([k] + [step for step, one in due if one is unit]), fn))
     return out
 
@@ -557,13 +557,17 @@
         def _():
             t = at - G1
             cols = pl.ds(pl.multiple_of(lax.div(t, 2) * 640, 128), 640)
-            for i in range(4):
-                rows = pl.ds(pl.multiple_of(lax.rem(t, 2) * 1024 + i * SPAN, SPAN), SPAN)
-                y = jnp.zeros((SPAN, 640), F32)
+
+            def part(i, _):
+                rows = pl.ds(pl.multiple_of(lax.rem(t, 2) * 1024 + i * 512, 512), 512)
+                y = jnp.zeros((512, 640), F32)
                 for c in THIRDS:
                     left = jnp.concatenate([act[c * 4 + q, rows, :] for q in range(4)], axis=1)
                     y = y + mm(left, wd_all[:, :, :, :, c * 64 : (c + 1) * 64, cols].reshape(CHUNK, 640))
                 a[rows, cols] = y.astype(BF16)
+                return NIL
+
+            lax.fori_loop(NIL, 2, part, NIL)
 
         @pl.when(at == D1)
         def _():
@@ -641,7 +645,7 @@
             units.append(Gather(here, wd_own.at[pl.ds(c * 64, 64)], wd_all.at[c], cuts(CUT_D, 1), sems, len(units) * n, c + 2))
         timed = list(zip((WIRE_GU, WIRE_D) * 2, units, strict=True))
         due = [(4, units[NIL]), (4, units[1]), (8, units[2]), (8, units[3])]
-        events = placed(wire_order(timed), [5.6] * UNITS, due)
+        events = placed(wire_order(timed), [5.6] * UNITS, due, 2 * EARLY_US)
         moves = ((a_in, a), (gu_first, gu_all.at[NIL]), (dy_in, dy), (wd_first, wd_all.at[NIL]))
         loads = [pltpu.make_async_copy(src, dst, local.at[i]) for i, (src, dst) in enumerate(moves)]
         spills = [pltpu.make_async_copy(gu_all.at[c], gu_rest.at[c - 1], local.at[3 + c]) for c in (1, 2)]
@@ -815,11 +819,11 @@
         for i in THIRDS:
             for n in PAIR:
                 taken = [pieces_in.pop(NIL) for _ in sums[i][n]]
-                g = jnp.concatenate([r[...].astype(F32) for r in taken], axis=1) if len(taken) > 1 else taken[NIL][...].astype(F32)
+                g = jnp.concatenate([r[...] for r in taken], axis=1) if len(taken) > 1 else taken[NIL][...]
                 if i < 2:
                     at = [c * CHUNK + k * 64 for k in range(16) for c in THIRDS]
                     g = jnp.concatenate([g[:, u : u + 64] for u in at], axis=1)
-                g = g * factor
+                g = g.astype(F32) * factor
                 m = 0.9 * ms[i][n] + 0.1 * g
                 v = 0.95 * vs[i][n] + 0.05 * g * g
                 w = ws[i][n].astype(F32)

time: 540 us -> 530 us (0.981); the launches traced: 532 us -> 529 us
  no operation moved by 1% of the time
where the time goes in v3:
time: 530 us; the launch traced here: 529 us
  Pallas kernels  528 us (100%)
    pallas_call x6, Pallas kernels, stage(): pl.pallas_call(kernel, grid=(steps,), in_specs=[spec for _, spec in args]...  290 us
    pallas_call x2, Pallas kernels, call(): pl.pallas_call(kernel, grid=(steps,), in_specs=[spec for _, spec in ins],...  223 us
    pallas_call x1, Pallas kernels, update_stage(): pl.pallas_call(kernel, grid=(steps,), in_specs=[pl.BlockSpec((8, 128), la...  15.2 us

profile of v3, /device:TPU:0, one launch (start us, length us, event | category | flops | bytes accessed | tf_op | source)
XLA Modules:
  0.0 528.7 jit_solution(13911093600248137290)
XLA Ops:
  0.6 132.9 %first.1 = (bf16[2,8,80,2048]{3,2,1,0:T(8,128)(2,1)}, f32[2048,3072]{1,0:T(8,128)}, f32[2048,3072]{1,0:T(8,128)}, bf16[2,8,192,2048]{3,2,1,0:T(8,128)(2,1)}, bf1...) custom-call(bf16[2048,1280]{1,0:T(8,128)(2,1)} %bitcast.8, ...), custom_call_target="tpu_custom_call" | custom-call | tf_op jit(solution)/shard_map/first/pallas_call | solution.py:477
  133.5 89.8 %second.1 = (bf16[2,2048,3072]{2,1,0:T(8,128)(2,1)}, bf16[2,8,192,2048]{3,2,1,0:T(8,128)(2,1)}, bf16[2,2,2,2,2,2,80,1024]{7,6,5,4,3,2,1,0:T(8,128)(2,1)}) custom-call(bf16[2048,1280]{1,0:T(8,128)(2,1)} %get-tuple-element.36.a_in, bf16[2048,1280]{1,0:T(8,128)(2,1)} %bitcast.4, bf16[2,80,3072]{2,1,0:T(8,128)(2,1)} %refs_1_.3, bf16[2,80,3072]{2,1,0:T(8,128)(2,1)} %refs_2_.1, ...), custom_call_target="tpu_custom_call" | custom-call | tf_op jit(solution)/shard_map/second/pallas_call | solution.py:477
  223.3 24.1 %dw.4.refs_2_ = f32[1,2,2,2,192,1280]{5,4,3,2,1,0:T(8,128)} custom-call(bf16[2,8,192,2048]{3,2,1,0:T(8,128)(2,1)} %get-tuple-element.43.refs_0_, bf16[1,2048,1280]{2,1,0:T(8,128)(2,1)} %refs_1_.2), custom_call_target="tpu_custom_call" | custom-call | tf_op jit(solution)/shard_map/dw/pallas_call | solution.py:331
  247.5 53.2 %dw.5 = (f32[2,2,2,2,80,3072]{5,4,3,2,1,0:T(8,128)}, bf16[192,1280]{1,0:T(8,128)(2,1)}) custom-call(bf16[2,8,80,2048]{3,2,1,0:T(8,128)(2,1)} %get-tuple-element.42.refs_0_, bf16[2,2048,3072]{2,1,0:T(8,128)(2,1)} %get-tuple-element.39.refs_1_.refs_0_, f32[1,2,2,2,192,1280]{5,4,3,2,1,0:T(8,128)} %dw.4.refs_2_), custom_call_target="tpu_custom_call" | custom-call | tf_op jit(solution)/shard_map/dw/pallas_call | solution.py:331
  300.7 51.4 %dinput.1 = (bf16[2048,1280]{1,0:T(8,128)(2,1)}, bf16[80,3072]{1,0:T(8,128)(2,1)}) custom-call(bf16[2,2048,3072]{2,1,0:T(8,128)(2,1)} %get-tuple-element.39.refs_1_.refs_0_, bf16[2,2,2,2,2,80,1024]{6,5,4,3,2,1,0:T(8,128)(2,1)} %get-tuple-element.37.gu_first.refs_1_, bf16[2,2,2,2,2,2,80,1024]{7,6,5,4,3,2,1,0:T(8,128)(2,1)} %get-tuple-element.40.refs_2_, ...), custom_call_target="tpu_custom_call" | custom-call | tf_op jit(solution)/shard_map/dinput/pallas_call | solution.py:331
  352.1 29.1 %dw.6 = (f32[1,2,2,2,192,1280]{5,4,3,2,1,0:T(8,128)}, bf16[80,1536]{1,0:T(8,128)(2,1)}) custom-call(bf16[2,8,192,2048]{3,2,1,0:T(8,128)(2,1)} %get-tuple-element.49.refs_0_, bf16[1,2048,1280]{2,1,0:T(8,128)(2,1)} %bitcast.6, f32[2,2,2,2,80,3072]{5,4,3,2,1,0:T(8,128)} %get-tuple-element.44.refs_5_.refs_2_.refs_4_), custom_call_target="tpu_custom_call" | custom-call | tf_op jit(solution)/shard_map/dw/pallas_call | solution.py:331
  381.2 45.7 %dact.1 = (bf16[2,2048,3072]{2,1,0:T(8,128)(2,1)}, bf16[80,1536]{1,0:T(8,128)(2,1)}, bf16[192,640]{1,0:T(8,128)(2,1)}) custom-call(bf16[2048,1280]{1,0:T(8,128)(2,1)} %get-tuple-element.45.refs_0_, bf16[16,192,1280]{2,1,0:T(8,128)(2,1)} %bitcast.7, f32[2048,3072]{1,0:T(8,128)} %get-tuple-element.47.refs_2_, f32[2048,3072]{1,0:T(8,128)} %get-tuple-element.48.refs_3_, ...), custom_call_target="tpu_custom_call" | custom-call | tf_op jit(solution)/shard_map/dact/pallas_call | solution.py:331
  426.9 86.4 %dw.7 = (bf16[192,640]{1,0:T(8,128)(2,1)}, bf16[80,3072]{1,0:T(8,128)(2,1)}, bf16[80,3072]{1,0:T(8,128)(2,1)}, f32[8,128]{1,0:T(8,128)}) custom-call(bf16[2,8,80,2048]{3,2,1,0:T(8,128)(2,1)} %get-tuple-element.35.refs_0_, bf16[2,2048,3072]{2,1,0:T(8,128)(2,1)} %get-tuple-element.51.refs_1_, f32[1,2,2,2,192,1280]{5,4,3,2,1,0:T(8,128)} %get-tuple-element.50.refs_5_.refs_2_, ...), custom_call_target="tpu_custom_call" | custom-call | tf_op jit(solution)/shard_map/dw/pallas_call | solution.py:331
  513.3 15.2 %update.1 = (bf16[2,80,3072]{2,1,0:T(8,128)(2,1)}, bf16[2,80,3072]{2,1,0:T(8,128)(2,1)}, bf16[2,192,1280]{2,1,0:T(8,128)(2,1)}, f32[2,80,3072]{2,1,0:T(8,128)}, ...) custom-call(f32[8,128]{1,0:T(8,128)} %get-tuple-element.57.refs_0_, ...), custom_call_target="tpu_custom_call" | custom-call | tf_op jit(solution)/shard_map/update/pallas_call | solution.py:843
